TPU v7x, 512 devices: a whole 4x4x16 slice. The times are simulated.
512 devices in a mesh: gx: 32 (over z, core), gy: 16 (over x, y).
Axes of the slice: x: 4, y: 4, z: 16, core: 2. Of those that a mesh axis runs over, the one named last changes fastest.
Arguments:
- load: float32 [32, 16, 320, 768], P('gx', 'gy'), may hold values from -6 to 6
- stiffness: bfloat16 [32, 16, 768, 768], P('gx', 'gy'), may hold values from -0.5 to 3, as said below
- local_inverse: bfloat16 [32, 16, 768, 768], P('gx', 'gy'), may hold values from -0.5 to 3, as said below
- phi: float32 [32, 16, 8, 768], P('gx', 'gy'), may hold values from -2.5 to 2.5
- level2_inverse: float32 [32, 128, 128], P('gx'), may hold values from -0.5 to 3, as said below
- level3_inverse: bfloat16 [512, 512], replicated, may hold values from -0.5 to 3, as said below
- aggregate: int32 [32, 16], P('gx', 'gy'), may hold values from 0 to 1
Outputs:
- solution: float32 [32, 16, 320, 768], P('gx', 'gy')
Inputs may be any that keep to these rules, and one draw needn't show every extreme that they name: `stiffness`: every block is symmetric positive definite. `local_inverse`: every block is symmetric positive definite. `level2_inverse`: every block is symmetric positive definite. `level3_inverse`: symmetric positive definite.
All inputs are finite; a program needn't handle non-finite values.
Results may differ from a plain program's by a relative error of at most 0.0091.
Values may be sent and summed in bfloat16 or wider, within the bound.
No kernel may reach another device: no remote copies, remote signals or barrier semaphores. Data moves between devices by JAX's collectives and lax.ppermute only.
A program may use at most 64 MiB of HBM per device.

v0:
```python
import functools

import jax
import jax.numpy as jnp
from jax import lax
from jax.sharding import Mesh
from jax.sharding import PartitionSpec as P

NAGG = 2
ITERS = 2
GX = ("gx_0", "gx_1")
GY = ("gy_0", "gy_1")
GX_GY = ("gx_0", "gx_1", "gy_0", "gy_1")


HIGH = lax.Precision.HIGHEST


def from_behind(value, axis, steps):
    count = lax.axis_size(axis)
    first, last = (max(0, -steps), min(count, count - steps))
    return lax.ppermute(value, axis, [(source, source + steps) for source in range(first, last)])


def joined_along(parts, dim):
    parts = jnp.moveaxis(parts, 0, dim)
    lengths = parts.shape
    return parts.reshape(*lengths[:dim], lengths[dim] * lengths[dim + 1], *lengths[dim + 2 :])


def copy_for_each(value, axis):
    copies = jnp.broadcast_to(value, (lax.axis_size(axis), *value.shape))
    return lax.all_to_all(copies, axis, split_axis=0, concat_axis=0, tiled=True)


def gather_directly(value, axis, dim):
    return joined_along(copy_for_each(value, axis), dim)


def by_axis(value, axes):
    return functools.reduce(lax.psum, axes, value)


def assemble(vec):
    rows, total = vec.shape
    width = total // 4
    edges = vec.reshape(rows, 4, width)
    west, east, south, north = (edges[:, 0], edges[:, 1], edges[:, 2], edges[:, 3])
    new_west = west + from_behind(east.astype(jnp.bfloat16), GX, 1).astype(east.dtype)
    new_east = east + from_behind(west.astype(jnp.bfloat16), GX, -1).astype(west.dtype)
    new_south = south + from_behind(north, GY, 1)
    new_north = north + from_behind(south, GY, -1)
    return jnp.stack([new_west, new_east, new_south, new_north], axis=1).reshape(rows, total)


def contract_last(left, right):
    return lax.dot_general(
        left, right, (((1,), (1,)), ((), ())), preferred_element_type=jnp.float32
    )


def contract_high(left, right):
    return lax.dot_general(
        left, right, (((1,), (1,)), ((), ())), precision=HIGH, preferred_element_type=jnp.float32
    )


def body(load, stiffness, local_inverse, phi, level2_inverse, level3_inverse, aggregate):
    load_here = load[0, 0]
    stiff = stiffness[0, 0]
    inverse = local_inverse[0, 0]
    basis = phi[0, 0]
    second_inv = level2_inverse[0]
    rows, total = load_here.shape
    width = total // 4
    primal_count = basis.shape[0]
    block = NAGG * primal_count
    col = lax.axis_index(GX)
    row = lax.axis_index(GY)
    cols_total = lax.axis_size(GX)
    rows_total = lax.axis_size(GY)
    edge_w = jnp.stack(
        [
            jnp.where(col > 0, 0.5, 1.0),
            jnp.where(col < cols_total - 1, 0.5, 1.0),
            jnp.where(row > 0, 0.5, 1.0),
            jnp.where(row < rows_total - 1, 0.5, 1.0),
        ]
    ).astype(jnp.float32)
    weights = jnp.repeat(edge_w, width)
    labels = jnp.arange(NAGG, dtype=jnp.int32)
    own_onehot = (aggregate[0, 0] == labels).astype(jnp.float32)
    members = gather_directly(aggregate[0], GY, 0)
    group_onehot = (members[:, None] == labels[None, :]).astype(jnp.float32)

    def apply(vec):
        return assemble(contract_last(vec.astype(jnp.bfloat16), stiff))

    def precondition(resid):
        scaled = weights * resid
        local = contract_last(scaled.astype(jnp.bfloat16), inverse)
        primal = contract_high(scaled, basis)
        grouped = gather_directly(primal, GY, 1)
        summed = jnp.einsum(
            "rbp,bq->rqp",
            grouped.reshape(rows, rows_total, primal_count),
            group_onehot,
            precision=HIGH,
        )
        summed = summed.reshape(rows, block)
        summed = summed.astype(jnp.bfloat16)
        second = contract_high(grouped, second_inv)
        second_own = lax.dynamic_slice_in_dim(second, row * primal_count, primal_count, 1)
        everyone = gather_directly(summed, GX, 1)
        mine = lax.dynamic_slice_in_dim(level3_inverse, col * block, block, 0)
        third = contract_last(everyone, mine)
        third_own = jnp.einsum(
            "rqp,q->rp", third.reshape(rows, NAGG, primal_count), own_onehot, precision=HIGH
        )
        full = local + jnp.dot(
            second_own + third_own, basis, precision=HIGH, preferred_element_type=jnp.float32
        )
        return assemble(weights * full)

    def inner(left, right):
        return jnp.sum(weights * left * right, axis=1)

    rhs = assemble(load_here)
    solution = jnp.zeros_like(rhs)
    resid = rhs

    def paired(resid, zvec, wvec):
        return (by_axis(inner(resid, zvec), GX_GY), by_axis(inner(zvec, wvec), GX_GY))

    zvec = precondition(resid)
    wvec = apply(zvec)
    gamma, delta = paired(resid, zvec, wvec)
    alpha = gamma / delta
    pvec, svec = (zvec, wvec)
    for step in range(ITERS):
        solution = solution + alpha[:, None] * pvec
        resid = resid - alpha[:, None] * svec
        if step < ITERS - 1:
            zvec = precondition(resid)
            wvec = apply(zvec)
            newer, delta = paired(resid, zvec, wvec)
            beta = newer / gamma
            alpha = newer / (delta - beta * newer / alpha)
            pvec = zvec + beta[:, None] * pvec
            svec = wvec + beta[:, None] * svec
            gamma = newer
    return solution[None, None]


def solution(mesh):
    finer = Mesh(mesh.devices.reshape(16, 2, 4, 4), ("gx_0", "gx_1", "gy_0", "gy_1"))
    return jax.shard_map(
        body,
        mesh=finer,
        in_specs=(
            P(GX, GY, None, None),
            P(GX, GY, None, None),
            P(GX, GY, None, None),
            P(GX, GY, None, None),
            P(GX, None, None),
            P(),
            P(GX, GY),
        ),
        out_specs=P(GX, GY, None, None),
        check_vma=False,
    )
```

profile of v0, /device:TPU:1, one launch (start us, length us, event | category | flops | bytes accessed | tf_op | source)
XLA Modules:
  0.0 326.3 jit_solution(14689023630016688939)
XLA Ops:
  0.0 1.7 copy.50
  1.7 4.0 %collective-permute-start.2 = (f32[320,192]{0,1:T(8,128)S(1)}, f32[320,192]{0,1:T(8,128)S(1)}, u32[]{:S(2)}, u32[]{:S(2)}) collective-permute-start(f32[320,192]{0,1:T(8,128)S(1)} %get-tuple-element.71), channel_id=1, source_target_pairs={{0,1},{1,2},{2,3},{3,4},{4,5},{5,6},{6,7},{7,8},{8,9},{9,10},{10,1... | collective-permute-start | bytes 737288 | tf_op jit(solution)/shard_map/ppermute | solution.py:22
  7.8 4.4 %collective-permute-start = (bf16[320,192]{0,1:T(8,128)(2,1)}, bf16[320,192]{0,1:T(8,128)(2,1)}, u32[]{:S(2)}, u32[]{:S(2)}) collective-permute-start(bf16[320,192]{0,1:T(8,128)(2,1)} %get-tuple-element.69), channel_id=1, source_target_pairs={{0,16},{16,32},{32,48},{48,64},{64,80},{80,96},{96,112},{112,128},... | collective-permute-start | bytes 368648 | tf_op jit(solution)/shard_map/ppermute | solution.py:22
  12.2 3.6 %collective-permute-start.1 = (bf16[320,192]{0,1:T(8,128)(2,1)}, bf16[320,192]{0,1:T(8,128)(2,1)}, u32[]{:S(2)}, u32[]{:S(2)}) collective-permute-start(bf16[320,192]{0,1:T(8,128)(2,1)} %get-tuple-element.70), channel_id=1, source_target_pairs={{16,0},{32,16},{48,32},{64,48},{80,64},{96,80},{112,96},{128,112},... | collective-permute-start | bytes 368648 | tf_op jit(solution)/shard_map/ppermute | solution.py:22
  17.0 6.2 %all-to-all-start.1 = ((s32[16,1,1]{2,1,0:T(1,128)}), s32[16,1,1]{2,1,0:T(1,128)}, u32[]{:S(2)}, u32[]{:S(2)}) async-start(s32[16,1,1]{2,1,0:T(1,128)} %broadcast_in_dim.26), calls=%async_computation.1 | async-start | bytes 16384 | tf_op jit(solution)/shard_map/all_to_all | solution.py:33
  26.4 3.1 all-to-all-done.1
  30.3 4.2 %all-to-all-start = ((f32[16,320,8]{1,2,0:T(8,128)}), f32[16,320,8]{1,2,0:T(8,128)}, u32[]{:S(2)}, u32[]{:S(2)}) async-start(f32[16,320,8]{1,2,0:T(8,128)} %broadcast_in_dim.25), calls=%async_computation | async-start | bytes 393216 | tf_op jit(solution)/shard_map/all_to_all | solution.py:33
  35.5 6.8 %all-to-all-done = f32[16,320,8]{1,2,0:T(8,128)} async-done(((f32[16,320,8]{1,2,0:T(8,128)}), f32[16,320,8]{1,2,0:T(8,128)}, u32[]{:S(2)}, u32[]{:S(2)}) %all-to-all-start) | async-done | bytes 163872 | tf_op jit(solution)/shard_map/all_to_all | solution.py:33
  44.2 18.5 %all-to-all-start.2 = ((bf16[32,320,16]{1,2,0:T(8,128)(2,1)}), bf16[32,320,16]{1,2,0:T(8,128)(2,1)}, u32[]{:S(2)}, u32[]{:S(2)}) async-start(bf16[32,320,16]{1,2,0:T(8,128)(2,1)} %broadcast_in_dim.27), calls=%async_computation.2 | async-start | bytes 786432 | tf_op jit(solution)/shard_map/all_to_all | solution.py:33
  63.0 2.7 fusion.5
  65.7 1.9 fusion.22
  67.6 23.0 %all-to-all-done.2 = bf16[32,320,16]{1,2,0:T(8,128)(2,1)} async-done(((bf16[32,320,16]{1,2,0:T(8,128)(2,1)}), bf16[32,320,16]{1,2,0:T(8,128)(2,1)}, u32[]{:S(2)}, u32[]{:S(2)}) %all-to-all-start.2) | async-done | bytes 327712 | tf_op jit(solution)/shard_map/all_to_all | solution.py:33
  91.8 2.3 fusion.38
  94.1 1.8 copy.68
  95.9 2.7 fusion.1
  100.2 2.2 collective-permute-start.6
  103.7 2.7 collective-permute-start.4
  106.4 1.9 collective-permute-start.5
  108.5 4.7 %collective-permute-done.5 = bf16[320,192]{0,1:T(8,128)(2,1)S(1)} collective-permute-done((bf16[320,192]{0,1:T(8,128)(2,1)S(1)}, bf16[320,192]{0,1:T(8,128)(2,1)S(1)}, u32[]{:S(2)}, u32[]{:S(2)}) %collective-permute-start.5) | collective-permute-done | bytes 122912 | tf_op jit(solution)/shard_map/ppermute | solution.py:22
  114.3 4.0 %collective-permute-start.10 = (f32[320,192]{0,1:T(8,128)S(1)}, f32[320,192]{0,1:T(8,128)S(1)}, u32[]{:S(2)}, u32[]{:S(2)}) collective-permute-start(f32[320,192]{0,1:T(8,128)S(1)} %get-tuple-element.55), channel_id=1, source_target_pairs={{0,1},{1,2},{2,3},{3,4},{4,5},{5,6},{6,7},{7,8},{8,9},{9,10},{10,1... | collective-permute-start | bytes 737288 | tf_op jit(solution)/shard_map/ppermute | solution.py:22
  119.6 2.0 collective-permute-start.8
  121.7 2.3 collective-permute-start.9
  124.0 4.5 %collective-permute-done.9 = bf16[320,192]{0,1:T(8,128)(2,1)S(1)} collective-permute-done((bf16[320,192]{0,1:T(8,128)(2,1)S(1)}, bf16[320,192]{0,1:T(8,128)(2,1)S(1)}, u32[]{:S(2)}, u32[]{:S(2)}) %collective-permute-start.9) | collective-permute-done | bytes 122912 | tf_op jit(solution)/shard_map/ppermute | solution.py:22
  130.6 20.6 %all-reduce.1 = (f32[320]{0:T(512)S(1)}, f32[320]{0:T(512)S(1)}) all-reduce(f32[320]{0:T(512)S(1)} %get-tuple-element.8, f32[320]{0:T(512)S(1)} %get-tuple-element.7), channel_id=1, replica_groups=mesh['gx_0'=16,'gx_1'=2,'gy_0'=4,'gy_1'=4] {'gx_0'}, use_global_device_ids=true, to_apply=%region_1.2 | all-reduce | flops 640 | bytes 5120 | tf_op jit(solution)/shard_map/psum | solution.py:41
  151.2 8.9 %all-reduce.7 = (f32[320]{0:T(512)S(1)}, f32[320]{0:T(512)S(1)}) all-reduce(f32[320]{0:T(512)S(1)} %get-tuple-element.11, f32[320]{0:T(512)S(1)} %get-tuple-element.12), channel_id=1, replica_groups=mesh['gx_0'=16,'gx_1'=2,'gy_0'=4,'gy_1'=4] {'gx_1'}, use_global_device_ids=true, to_apply=%region_2.3 | all-reduce | flops 640 | bytes 5120 | tf_op jit(solution)/shard_map/psum | solution.py:41
  160.1 12.1 %all-reduce.5 = (f32[320]{0:T(512)S(1)}, f32[320]{0:T(512)S(1)}) all-reduce(f32[320]{0:T(512)S(1)} %get-tuple-element.23, f32[320]{0:T(512)S(1)} %get-tuple-element.24), channel_id=1, replica_groups=mesh['gx_0'=16,'gx_1'=2,'gy_0'=4,'gy_1'=4] {'gy_0'}, use_global_device_ids=true, to_apply=%region_3.4 | all-reduce | flops 640 | bytes 5120 | tf_op jit(solution)/shard_map/psum | solution.py:41
  172.2 6.2 %all-reduce.3 = (f32[320]{0:T(512)S(1)}, f32[320]{0:T(512)S(1)}) all-reduce(f32[320]{0:T(512)S(1)} %get-tuple-element.19, f32[320]{0:T(512)S(1)} %get-tuple-element.20), channel_id=1, replica_groups=mesh['gx_0'=16,'gx_1'=2,'gy_0'=4,'gy_1'=4] {'gy_1'}, use_global_device_ids=true, to_apply=%region_4.5 | all-reduce | flops 640 | bytes 5120 | tf_op jit(solution)/shard_map/psum | solution.py:41
  179.0 2.4 fusion.66
  182.2 10.1 %all_to_all.26 = f32[16,320,8]{1,2,0:T(8,128)S(1)} all-to-all(f32[16,320,8]{1,2,0:T(8,128)S(1)} %broadcast_in_dim.28), channel_id=1, replica_groups=mesh['gx_0'=16,'gx_1'=2,'gy_0'=4,'gy_1'=4] {'gy_0','gy_1'}, dimensions={0} | all-to-all | bytes 327680 | tf_op jit(solution)/shard_map/all_to_all | solution.py:33
  194.0 11.2 %all-to-all-start.4 = ((bf16[32,320,16]{1,2,0:T(8,128)(2,1)}), bf16[32,320,16]{1,2,0:T(8,128)(2,1)}, u32[]{:S(2)}, u32[]{:S(2)}) async-start(bf16[32,320,16]{1,2,0:T(8,128)(2,1)} %broadcast_in_dim.29), calls=%async_computation.4 | async-start | bytes 786432 | tf_op jit(solution)/shard_map/all_to_all | solution.py:33
  205.2 2.7 fusion.3
  208.9 24.0 %all-to-all-done.4 = bf16[32,320,16]{1,2,0:T(8,128)(2,1)} async-done(((bf16[32,320,16]{1,2,0:T(8,128)(2,1)}), bf16[32,320,16]{1,2,0:T(8,128)(2,1)}, u32[]{:S(2)}, u32[]{:S(2)}) %all-to-all-start.4) | async-done | bytes 327712 | tf_op jit(solution)/shard_map/all_to_all | solution.py:33
  234.1 2.3 fusion.36
  236.4 1.8 copy.72
  238.2 2.6 fusion
  242.5 2.2 collective-permute-start.14
  246.0 2.7 collective-permute-start.12
  248.7 1.9 collective-permute-start.13
  250.8 4.7 %collective-permute-done.13 = bf16[320,192]{0,1:T(8,128)(2,1)S(1)} collective-permute-done((bf16[320,192]{0,1:T(8,128)(2,1)S(1)}, bf16[320,192]{0,1:T(8,128)(2,1)S(1)}, u32[]{:S(2)}, u32[]{:S(2)}) %collective-permute-start.13) | collective-permute-done | bytes 122912 | tf_op jit(solution)/shard_map/ppermute | solution.py:22
  257.5 4.7 %collective-permute-start.18 = (f32[320,192]{0,1:T(8,128)}, f32[320,192]{0,1:T(8,128)}, u32[]{:S(2)}, u32[]{:S(2)}) collective-permute-start(f32[320,192]{0,1:T(8,128)} %get-tuple-element.38), channel_id=1, source_target_pairs={{0,1},{1,2},{2,3},{3,4},{4,5},{5,6},{6,7},{7,8},{8,9},{9,10},{10,1... | collective-permute-start | bytes 737288 | tf_op jit(solution)/shard_map/ppermute | solution.py:22
  264.3 2.0 collective-permute-start.16
  266.3 2.9 collective-permute-start.17
  269.3 2.6 copy.57
  276.3 21.0 %all-reduce = (f32[320]{0:T(512)S(1)}, f32[320]{0:T(512)S(1)}) all-reduce(f32[320]{0:T(512)S(1)} %get-tuple-element.6, f32[320]{0:T(512)S(1)} %get-tuple-element.5), channel_id=1, replica_groups=mesh['gx_0'=16,'gx_1'=2,'gy_0'=4,'gy_1'=4] {'gx_0'}, use_global_device_ids=true, to_apply=%region_11.12 | all-reduce | flops 640 | bytes 5120 | tf_op jit(solution)/shard_map/psum | solution.py:41
  297.3 8.4 %all-reduce.6 = (f32[320]{0:T(512)S(1)}, f32[320]{0:T(512)S(1)}) all-reduce(f32[320]{0:T(512)S(1)} %get-tuple-element.9, f32[320]{0:T(512)S(1)} %get-tuple-element.10), channel_id=1, replica_groups=mesh['gx_0'=16,'gx_1'=2,'gy_0'=4,'gy_1'=4] {'gx_1'}, use_global_device_ids=true, to_apply=%region_12.13 | all-reduce | flops 640 | bytes 5120 | tf_op jit(solution)/shard_map/psum | solution.py:41
  305.8 12.1 %all-reduce.4 = (f32[320]{0:T(512)S(1)}, f32[320]{0:T(512)S(1)}) all-reduce(f32[320]{0:T(512)S(1)} %get-tuple-element.21, f32[320]{0:T(512)S(1)} %get-tuple-element.22), channel_id=1, replica_groups=mesh['gx_0'=16,'gx_1'=2,'gy_0'=4,'gy_1'=4] {'gy_0'}, use_global_device_ids=true, to_apply=%region_13.14 | all-reduce | flops 640 | bytes 5120 | tf_op jit(solution)/shard_map/psum | solution.py:41
  317.9 6.0 %all-reduce.2 = (f32[320]{0:T(512)S(1)}, f32[320]{0:T(512)S(1)}) all-reduce(f32[320]{0:T(512)S(1)} %get-tuple-element.17, f32[320]{0:T(512)S(1)} %get-tuple-element.18), channel_id=1, replica_groups=mesh['gx_0'=16,'gx_1'=2,'gy_0'=4,'gy_1'=4] {'gy_1'}, use_global_device_ids=true, to_apply=%region_14.15 | all-reduce | flops 640 | bytes 5120 | tf_op jit(solution)/shard_map/psum | solution.py:41
  323.9 2.4 multiply_add_fusion
  (147 shorter events, 35.1 us)
Async XLA Ops:
  0.0 113.5 %copy-start = (bf16[1,1,768,768]{3,2,1,0:T(8,128)(2,1)S(1)}, bf16[1,1,768,768]{3,2,1,0:T(8,128)(2,1)}, u32[]{:S(2)}) copy-start(bf16[1,1,768,768]{3,2,1,0:T(8,128)(2,1)} %param.8) | copy-start | bytes 3538948
  1.7 21.6 %collective-permute-start.2 = (f32[320,192]{0,1:T(8,128)S(1)}, f32[320,192]{0,1:T(8,128)S(1)}, u32[]{:S(2)}, u32[]{:S(2)}) collective-permute-start(f32[320,192]{0,1:T(8,128)S(1)} %get-tuple-element.71), channel_id=1, source_target_pairs={{0,1},{1,2},{2,3},{3,4},{4,5},{5,6},{6,7},{7,8},{8,9},{9,10},{10,1... | collective-permute-start | bytes 737288 | tf_op jit(solution)/shard_map/ppermute | solution.py:22
  5.8 17.6 %collective-permute-start.3 = (f32[320,192]{0,1:T(8,128)S(1)}, f32[320,192]{0,1:T(8,128)S(1)}, u32[]{:S(2)}, u32[]{:S(2)}) collective-permute-start(f32[320,192]{0,1:T(8,128)S(1)} %get-tuple-element.72), channel_id=1, source_target_pairs={{1,0},{2,1},{3,2},{4,3},{5,4},{6,5},{7,6},{8,7},{9,8},{10,9},{11,1... | collective-permute-start | bytes 737288 | tf_op jit(solution)/shard_map/ppermute | solution.py:22
  7.8 15.5 %collective-permute-start = (bf16[320,192]{0,1:T(8,128)(2,1)}, bf16[320,192]{0,1:T(8,128)(2,1)}, u32[]{:S(2)}, u32[]{:S(2)}) collective-permute-start(bf16[320,192]{0,1:T(8,128)(2,1)} %get-tuple-element.69), channel_id=1, source_target_pairs={{0,16},{16,32},{32,48},{48,64},{64,80},{80,96},{96,112},{112,128},... | collective-permute-start | bytes 368648 | tf_op jit(solution)/shard_map/ppermute | solution.py:22
  12.2 11.1 %collective-permute-start.1 = (bf16[320,192]{0,1:T(8,128)(2,1)}, bf16[320,192]{0,1:T(8,128)(2,1)}, u32[]{:S(2)}, u32[]{:S(2)}) collective-permute-start(bf16[320,192]{0,1:T(8,128)(2,1)} %get-tuple-element.70), channel_id=1, source_target_pairs={{16,0},{32,16},{48,32},{64,48},{80,64},{96,80},{112,96},{128,112},... | collective-permute-start | bytes 368648 | tf_op jit(solution)/shard_map/ppermute | solution.py:22
  17.0 12.6 %all-to-all-start.1 = ((s32[16,1,1]{2,1,0:T(1,128)}), s32[16,1,1]{2,1,0:T(1,128)}, u32[]{:S(2)}, u32[]{:S(2)}) async-start(s32[16,1,1]{2,1,0:T(1,128)} %broadcast_in_dim.26), calls=%async_computation.1 | async-start | bytes 16384 | tf_op jit(solution)/shard_map/all_to_all | solution.py:33
  26.4 36.5 %copy-start.1 = (bf16[1,1,768,768]{3,2,1,0:T(8,128)(2,1)S(1)}, bf16[1,1,768,768]{3,2,1,0:T(8,128)(2,1)}, u32[]{:S(2)}) copy-start(bf16[1,1,768,768]{3,2,1,0:T(8,128)(2,1)} %param.9) | copy-start | bytes 3538948
  30.3 12.0 %all-to-all-start = ((f32[16,320,8]{1,2,0:T(8,128)}), f32[16,320,8]{1,2,0:T(8,128)}, u32[]{:S(2)}, u32[]{:S(2)}) async-start(f32[16,320,8]{1,2,0:T(8,128)} %broadcast_in_dim.25), calls=%async_computation | async-start | bytes 393216 | tf_op jit(solution)/shard_map/all_to_all | solution.py:33
  35.5 27.3 %copy-start.38 = (s32[16]{0:T(128)}, s32[16]{0:T(128)S(1)}, u32[]{:S(2)}) copy-start(s32[16]{0:T(128)S(1)} %reduce.4) | copy-start | bytes 196
  44.2 46.4 %all-to-all-start.2 = ((bf16[32,320,16]{1,2,0:T(8,128)(2,1)}), bf16[32,320,16]{1,2,0:T(8,128)(2,1)}, u32[]{:S(2)}, u32[]{:S(2)}) async-start(bf16[32,320,16]{1,2,0:T(8,128)(2,1)} %broadcast_in_dim.27), calls=%async_computation.2 | async-start | bytes 786432 | tf_op jit(solution)/shard_map/all_to_all | solution.py:33
  63.0 2.7 copy-start.32
  91.8 4.1 %copy-start.5 = (f32[320,768]{1,0:T(8,128)S(1)}, f32[320,768]{1,0:T(8,128)}, u32[]{:S(2)}) copy-start(f32[320,768]{1,0:T(8,128)} %fusion.5) | copy-start | bytes 2949124
  91.8 4.1 %copy-start.29 = (f32[1,1,8,768]{3,2,1,0:T(8,128)S(1)}, f32[1,1,8,768]{3,2,1,0:T(8,128)}, u32[]{:S(2)}) copy-start(f32[1,1,8,768]{3,2,1,0:T(8,128)} %param.10) | copy-start | bytes 73732
  100.2 13.0 %collective-permute-start.6 = (f32[320,192]{0,1:T(8,128)S(1)}, f32[320,192]{0,1:T(8,128)S(1)}, u32[]{:S(2)}, u32[]{:S(2)}) collective-permute-start(f32[320,192]{0,1:T(8,128)S(1)} %get-tuple-element.63), channel_id=1, source_target_pairs={{0,1},{1,2},{2,3},{3,4},{4,5},{5,6},{6,7},{7,8},{8,9},{9,10},{10,1... | collective-permute-start | bytes 737288 | tf_op jit(solution)/shard_map/ppermute | solution.py:22
  102.4 10.8 %collective-permute-start.7 = (f32[320,192]{0,1:T(8,128)S(1)}, f32[320,192]{0,1:T(8,128)S(1)}, u32[]{:S(2)}, u32[]{:S(2)}) collective-permute-start(f32[320,192]{0,1:T(8,128)S(1)} %get-tuple-element.64), channel_id=1, source_target_pairs={{1,0},{2,1},{3,2},{4,3},{5,4},{6,5},{7,6},{8,7},{9,8},{10,9},{11,1... | collective-permute-start | bytes 737288 | tf_op jit(solution)/shard_map/ppermute | solution.py:22
  103.7 4.7 %collective-permute-start.4 = (bf16[320,192]{0,1:T(8,128)(2,1)S(1)}, bf16[320,192]{0,1:T(8,128)(2,1)S(1)}, u32[]{:S(2)}, u32[]{:S(2)}) collective-permute-start(bf16[320,192]{0,1:T(8,128)(2,1)S(1)} %get-tuple-element.61), channel_id=1, source_target_pairs={{0,16},{16,32},{32,48},{48,64},{64,80},{80,96},{96,112},{112,128},... | collective-permute-start | bytes 368648 | tf_op jit(solution)/shard_map/ppermute | solution.py:22
  106.4 6.8 %collective-permute-start.5 = (bf16[320,192]{0,1:T(8,128)(2,1)S(1)}, bf16[320,192]{0,1:T(8,128)(2,1)S(1)}, u32[]{:S(2)}, u32[]{:S(2)}) collective-permute-start(bf16[320,192]{0,1:T(8,128)(2,1)S(1)} %get-tuple-element.62), channel_id=1, source_target_pairs={{16,0},{32,16},{48,32},{64,48},{80,64},{96,80},{112,96},{128,112},... | collective-permute-start | bytes 368648 | tf_op jit(solution)/shard_map/ppermute | solution.py:22
  114.3 14.2 %collective-permute-start.10 = (f32[320,192]{0,1:T(8,128)S(1)}, f32[320,192]{0,1:T(8,128)S(1)}, u32[]{:S(2)}, u32[]{:S(2)}) collective-permute-start(f32[320,192]{0,1:T(8,128)S(1)} %get-tuple-element.55), channel_id=1, source_target_pairs={{0,1},{1,2},{2,3},{3,4},{4,5},{5,6},{6,7},{7,8},{8,9},{9,10},{10,1... | collective-permute-start | bytes 737288 | tf_op jit(solution)/shard_map/ppermute | solution.py:22
  118.3 10.7 %collective-permute-start.11 = (f32[320,192]{0,1:T(8,128)S(1)}, f32[320,192]{0,1:T(8,128)S(1)}, u32[]{:S(2)}, u32[]{:S(2)}) collective-permute-start(f32[320,192]{0,1:T(8,128)S(1)} %get-tuple-element.56), channel_id=1, source_target_pairs={{1,0},{2,1},{3,2},{4,3},{5,4},{6,5},{7,6},{8,7},{9,8},{10,9},{11,1... | collective-permute-start | bytes 737288 | tf_op jit(solution)/shard_map/ppermute | solution.py:22
  119.6 4.3 %collective-permute-start.8 = (bf16[320,192]{0,1:T(8,128)(2,1)S(1)}, bf16[320,192]{0,1:T(8,128)(2,1)S(1)}, u32[]{:S(2)}, u32[]{:S(2)}) collective-permute-start(bf16[320,192]{0,1:T(8,128)(2,1)S(1)} %get-tuple-element.53), channel_id=1, source_target_pairs={{0,16},{16,32},{32,48},{48,64},{64,80},{80,96},{96,112},{112,128},... | collective-permute-start | bytes 368648 | tf_op jit(solution)/shard_map/ppermute | solution.py:22
  121.7 6.8 %collective-permute-start.9 = (bf16[320,192]{0,1:T(8,128)(2,1)S(1)}, bf16[320,192]{0,1:T(8,128)(2,1)S(1)}, u32[]{:S(2)}, u32[]{:S(2)}) collective-permute-start(bf16[320,192]{0,1:T(8,128)(2,1)S(1)} %get-tuple-element.54), channel_id=1, source_target_pairs={{16,0},{32,16},{48,32},{64,48},{80,64},{96,80},{112,96},{128,112},... | collective-permute-start | bytes 368648 | tf_op jit(solution)/shard_map/ppermute | solution.py:22
  129.1 49.8 %copy-start.15 = (f32[320,1,192]{0,2,1:T(8,128)S(1)}, f32[320,1,192]{0,2,1:T(8,128)}, u32[]{:S(2)}) copy-start(f32[320,1,192]{0,2,1:T(8,128)} %copy-done.14) | copy-start | bytes 737284
  129.1 49.8 %copy-start.17 = (f32[320,1,192]{0,2,1:T(8,128)S(1)}, f32[320,1,192]{0,2,1:T(8,128)}, u32[]{:S(2)}) copy-start(f32[320,1,192]{0,2,1:T(8,128)} %copy-done.16) | copy-start | bytes 737284
  129.1 49.8 %copy-start.19 = (f32[320,1,192]{0,2,1:T(8,128)S(1)}, f32[320,1,192]{0,2,1:T(8,128)}, u32[]{:S(2)}) copy-start(f32[320,1,192]{0,2,1:T(8,128)} %copy-done.18) | copy-start | bytes 737284
  129.2 49.8 %copy-start.21 = (f32[320,1,192]{0,2,1:T(8,128)S(1)}, f32[320,1,192]{0,2,1:T(8,128)}, u32[]{:S(2)}) copy-start(f32[320,1,192]{0,2,1:T(8,128)} %copy-done.20) | copy-start | bytes 737284
  178.4 3.0 copy-start.34
  181.4 11.6 %copy-start.39 = (s32[16]{0:T(128)S(1)}, s32[16]{0:T(128)}, u32[]{:S(2)}) copy-start(s32[16]{0:T(128)} %copy-done.38) | copy-start | bytes 196
  182.1 23.1 %copy-start.2 = (bf16[1,1,768,768]{3,2,1,0:T(8,128)(2,1)S(1)}, bf16[1,1,768,768]{3,2,1,0:T(8,128)(2,1)}, u32[]{:S(2)}) copy-start(bf16[1,1,768,768]{3,2,1,0:T(8,128)(2,1)} %param.9) | copy-start | bytes 3538948
  194.0 39.0 %all-to-all-start.4 = ((bf16[32,320,16]{1,2,0:T(8,128)(2,1)}), bf16[32,320,16]{1,2,0:T(8,128)(2,1)}, u32[]{:S(2)}, u32[]{:S(2)}) async-start(bf16[32,320,16]{1,2,0:T(8,128)(2,1)} %broadcast_in_dim.29), calls=%async_computation.4 | async-start | bytes 786432 | tf_op jit(solution)/shard_map/all_to_all | solution.py:33
  205.2 2.7 copy-start.27
  205.2 2.7 copy-start.33
  234.1 4.1 %copy-start.4 = (f32[320,768]{1,0:T(8,128)S(1)}, f32[320,768]{1,0:T(8,128)}, u32[]{:S(2)}) copy-start(f32[320,768]{1,0:T(8,128)} %fusion.3) | copy-start | bytes 2949124
  234.1 4.1 %copy-start.31 = (f32[1,1,8,768]{3,2,1,0:T(8,128)S(1)}, f32[1,1,8,768]{3,2,1,0:T(8,128)}, u32[]{:S(2)}) copy-start(f32[1,1,8,768]{3,2,1,0:T(8,128)} %param.10) | copy-start | bytes 73732
  242.5 13.0 %collective-permute-start.14 = (f32[320,192]{0,1:T(8,128)S(1)}, f32[320,192]{0,1:T(8,128)S(1)}, u32[]{:S(2)}, u32[]{:S(2)}) collective-permute-start(f32[320,192]{0,1:T(8,128)S(1)} %get-tuple-element.47), channel_id=1, source_target_pairs={{0,1},{1,2},{2,3},{3,4},{4,5},{5,6},{6,7},{7,8},{8,9},{9,10},{10,1... | collective-permute-start | bytes 737288 | tf_op jit(solution)/shard_map/ppermute | solution.py:22
  244.6 10.8 %collective-permute-start.15 = (f32[320,192]{0,1:T(8,128)S(1)}, f32[320,192]{0,1:T(8,128)S(1)}, u32[]{:S(2)}, u32[]{:S(2)}) collective-permute-start(f32[320,192]{0,1:T(8,128)S(1)} %get-tuple-element.48), channel_id=1, source_target_pairs={{1,0},{2,1},{3,2},{4,3},{5,4},{6,5},{7,6},{8,7},{9,8},{10,9},{11,1... | collective-permute-start | bytes 737288 | tf_op jit(solution)/shard_map/ppermute | solution.py:22
  246.0 4.8 %collective-permute-start.12 = (bf16[320,192]{0,1:T(8,128)(2,1)S(1)}, bf16[320,192]{0,1:T(8,128)(2,1)S(1)}, u32[]{:S(2)}, u32[]{:S(2)}) collective-permute-start(bf16[320,192]{0,1:T(8,128)(2,1)S(1)} %get-tuple-element.45), channel_id=1, source_target_pairs={{0,16},{16,32},{32,48},{48,64},{64,80},{80,96},{96,112},{112,128},... | collective-permute-start | bytes 368648 | tf_op jit(solution)/shard_map/ppermute | solution.py:22
  248.7 6.8 %collective-permute-start.13 = (bf16[320,192]{0,1:T(8,128)(2,1)S(1)}, bf16[320,192]{0,1:T(8,128)(2,1)S(1)}, u32[]{:S(2)}, u32[]{:S(2)}) collective-permute-start(bf16[320,192]{0,1:T(8,128)(2,1)S(1)} %get-tuple-element.46), channel_id=1, source_target_pairs={{16,0},{32,16},{48,32},{64,48},{80,64},{96,80},{112,96},{128,112},... | collective-permute-start | bytes 368648 | tf_op jit(solution)/shard_map/ppermute | solution.py:22
  257.5 15.8 %collective-permute-start.18 = (f32[320,192]{0,1:T(8,128)}, f32[320,192]{0,1:T(8,128)}, u32[]{:S(2)}, u32[]{:S(2)}) collective-permute-start(f32[320,192]{0,1:T(8,128)} %get-tuple-element.38), channel_id=1, source_target_pairs={{0,1},{1,2},{2,3},{3,4},{4,5},{5,6},{6,7},{7,8},{8,9},{9,10},{10,1... | collective-permute-start | bytes 737288 | tf_op jit(solution)/shard_map/ppermute | solution.py:22
  262.2 11.1 %collective-permute-start.19 = (f32[320,192]{0,1:T(8,128)}, f32[320,192]{0,1:T(8,128)}, u32[]{:S(2)}, u32[]{:S(2)}) collective-permute-start(f32[320,192]{0,1:T(8,128)} %get-tuple-element.39), channel_id=1, source_target_pairs={{1,0},{2,1},{3,2},{4,3},{5,4},{6,5},{7,6},{8,7},{9,8},{10,9},{11,1... | collective-permute-start | bytes 737288 | tf_op jit(solution)/shard_map/ppermute | solution.py:22
  264.3 7.6 %collective-permute-start.16 = (bf16[320,192]{0,1:T(8,128)(2,1)}, bf16[320,192]{0,1:T(8,128)(2,1)}, u32[]{:S(2)}, u32[]{:S(2)}) collective-permute-start(bf16[320,192]{0,1:T(8,128)(2,1)} %get-tuple-element.36), channel_id=1, source_target_pairs={{0,16},{16,32},{32,48},{48,64},{64,80},{80,96},{96,112},{112,128},... | collective-permute-start | bytes 368648 | tf_op jit(solution)/shard_map/ppermute | solution.py:22
  266.3 6.9 %collective-permute-start.17 = (bf16[320,192]{0,1:T(8,128)(2,1)}, bf16[320,192]{0,1:T(8,128)(2,1)}, u32[]{:S(2)}, u32[]{:S(2)}) collective-permute-start(bf16[320,192]{0,1:T(8,128)(2,1)} %get-tuple-element.37), channel_id=1, source_target_pairs={{16,0},{32,16},{48,32},{64,48},{80,64},{96,80},{112,96},{128,112},... | collective-permute-start | bytes 368648 | tf_op jit(solution)/shard_map/ppermute | solution.py:22
  271.8 2.7 copy-start.7
  271.8 2.7 copy-start.9
  271.8 2.7 copy-start.11
  271.8 2.7 copy-start.13
  275.0 48.9 %copy-start.35 = (f32[320]{0:T(512)S(1)}, f32[320]{0:T(512)}, u32[]{:S(2)}) copy-start(f32[320]{0:T(512)} %copy-done.34) | copy-start | bytes 3844
  275.0 48.9 %copy-start.37 = (f32[320]{0:T(512)S(1)}, f32[320]{0:T(512)}, u32[]{:S(2)}) copy-start(f32[320]{0:T(512)} %copy-done.36) | copy-start | bytes 3844
  275.0 48.9 %copy-start.3 = (f32[1,1,320,768]{3,2,1,0:T(8,128)S(1)}, f32[1,1,320,768]{3,2,1,0:T(8,128)}, u32[]{:S(2)}) copy-start(f32[1,1,320,768]{3,2,1,0:T(8,128)} %copy.57) | copy-start | bytes 2949124
  (16 other events, 19.7 us)
where the time goes:
time: 331 us; the launch traced here: 326 us
  blocking collectives  106 us (32%)
  starting transfers between devices  90.1 us (27%)
  waiting for transfers between devices  72.9 us (22%)
  matrix products  24.9 us (8%)
  local copies, waits for them, and re-layouts  19.4 us (6%)
  other arithmetic  12 us (4%)
    psum x8, blocking collectives, by_axis(): return functools.reduce(lax.psum, axes, value)  95.4 us
    all_to_all x4, waiting for transfers between devices, copy_for_each(): return lax.all_to_all(copies, axis, split_axis=0, concat_axis=0, tiled=True)  56.9 us
    ppermute x20, starting transfers between devices, from_behind(): lax.ppermute(value, axis, [(source, source + steps) for source in range(f...  50 us
    all_to_all x4, starting transfers between devices, copy_for_each(): return lax.all_to_all(copies, axis, split_axis=0, concat_axis=0, tiled=True)  40.1 us
    ppermute x20, waiting for transfers between devices, from_behind(): lax.ppermute(value, axis, [(source, source + steps) for source in range(f...  16.1 us
    all_to_all x1, blocking collectives, copy_for_each(): return lax.all_to_all(copies, axis, split_axis=0, concat_axis=0, tiled=True)  10.1 us
    dot_general x6, matrix products, contract_last(): lax.dot_general(left, right, (((1,), (1,)), ((), ())), preferred_element_...  9.32 us
  transfers between devices with their start and end apart: 24, of which 11 were waited for; matrix products, arithmetic and copies ran while one was open for 5% of the time, Pallas kernels for 0%

commit v1 on v0

v1 whole, which is shorter than its diff:
```python
import jax
import jax.numpy as jnp
from jax import lax
from jax.sharding import Mesh
from jax.sharding import PartitionSpec as P

NAGG = 2
GX = ("gx_0", "gx_1")
GY = ("gy_0", "gy_1")
PLANE = ("gx_1", "gy_0", "gy_1")
DEPTH = ("gx_0",)

HIGH = lax.Precision.HIGHEST


def from_behind(value, axis, steps):
    count = lax.axis_size(axis)
    first, last = (max(0, -steps), min(count, count - steps))
    return lax.ppermute(value, axis, [(source, source + steps) for source in range(first, last)])


def exchange(parts, axis):
    return lax.all_to_all(parts, axis, split_axis=0, concat_axis=0, tiled=True)


def copies(value, axis):
    return exchange(jnp.broadcast_to(value, (lax.axis_size(axis), *value.shape)), axis)


def assemble(vec):
    width = vec.shape[0] // 4
    west, east, south, north = (vec[k * width : (k + 1) * width] for k in range(4))
    narrow = vec.astype(jnp.bfloat16)
    west_n, east_n, south_n, north_n = (narrow[k * width : (k + 1) * width] for k in range(4))
    new_west = west + from_behind(east_n, GX, 1).astype(vec.dtype)
    new_east = east + from_behind(west_n, GX, -1).astype(vec.dtype)
    new_south = south + from_behind(north_n, GY, 1).astype(vec.dtype)
    new_north = north + from_behind(south_n, GY, -1).astype(vec.dtype)
    return jnp.concatenate([new_west, new_east, new_south, new_north], axis=0)


def halves(value):
    upper = lax.reduce_precision(value, 8, 7)
    return (upper.astype(jnp.bfloat16), (value - upper).astype(jnp.bfloat16))


def times(left, right):
    return lax.dot_general(
        left, right, (((1,), (0,)), ((), ())), preferred_element_type=jnp.float32
    )


def times_high(left, right):
    return lax.dot_general(
        left,
        right,
        (((1,), (0,)), ((), ())),
        precision=HIGH,
        preferred_element_type=jnp.float32,
    )


def body(load, stiffness, local_inverse, phi, level2_inverse, level3_inverse, aggregate):
    load_here = load[0, 0].T
    stiff = stiffness[0, 0]
    inverse = local_inverse[0, 0]
    basis = phi[0, 0]
    second_inv = level2_inverse[0]
    total, rows = load_here.shape
    width = total // 4
    count = basis.shape[0]
    block = NAGG * count
    col = lax.axis_index(GX)
    row = lax.axis_index(GY)
    cols_total = lax.axis_size(GX)
    rows_total = lax.axis_size(GY)
    share = rows // rows_total
    edge_w = jnp.stack(
        [
            jnp.where(col > 0, 0.5, 1.0),
            jnp.where(col < cols_total - 1, 0.5, 1.0),
            jnp.where(row > 0, 0.5, 1.0),
            jnp.where(row < rows_total - 1, 0.5, 1.0),
        ]
    ).astype(jnp.float32)
    weights = jnp.repeat(edge_w, width)[:, None]
    own = aggregate[0, 0]
    mine = lax.dynamic_slice_in_dim(level3_inverse, col * block, block, 0).astype(jnp.float32)
    basis_hi, basis_lo = halves(basis)
    spread = jnp.concatenate([basis_hi, basis_lo, basis_hi], axis=0).T

    def scatter(value):
        lead = value.shape[0]
        parts = value.reshape(lead, rows_total, share).transpose(1, 0, 2)
        return exchange(parts, GY)

    def gather(parts):
        back = exchange(parts, GY)
        return back.transpose(1, 0, 2).reshape(back.shape[1], rows)

    def precondition(scaled, extra):
        primal = times_high(basis, scaled)
        masked = [jnp.where(own == label, primal, 0.0) for label in range(NAGG)]
        kept = 0 if extra is None else extra.shape[0]
        message = jnp.concatenate(masked if extra is None else [*masked, extra], axis=0)
        local = times(inverse, scaled.astype(jnp.bfloat16))
        group = scatter(message)
        grouped = sum(group[:, q * count : (q + 1) * count] for q in range(NAGG))
        grouped = grouped.reshape(rows_total * count, share)
        everyone = copies(jnp.sum(group, axis=0), GX)
        second = times_high(second_inv, grouped).reshape(rows_total, 1, count, share)
        summed = everyone[:, :block].reshape(cols_total * block, share)
        third = times_high(mine, summed).reshape(1, NAGG, count, share)
        answer = (second + third).reshape(rows_total, block, share)
        if kept:
            sums = jnp.sum(everyone[:, block:], axis=0)
            sums = jnp.broadcast_to(sums, (rows_total, kept, share))
            answer = jnp.concatenate([answer, sums], axis=1)
        result = gather(answer)
        coarse = result[:count]
        for label in range(1, NAGG):
            coarse = jnp.where(own == label, result[label * count : (label + 1) * count], coarse)
        coarse_hi, coarse_lo = halves(coarse)
        stacked = jnp.concatenate([coarse_hi, coarse_hi, coarse_lo], axis=0)
        full = local + times(spread, stacked)
        return (assemble(weights * full), result[block:])

    def apply(vec):
        return times(stiff, vec.astype(jnp.bfloat16))

    def inner(left, right):
        return jnp.sum(left * right, axis=0)

    rhs = weights * assemble(load_here)
    zero, _ = precondition(rhs, None)
    image = apply(zero)
    dots = jnp.stack([inner(rhs, zero), inner(zero, image)])
    scaled = weights * assemble(image)
    other, dots = precondition(scaled, dots)
    gamma, delta = (dots[0], dots[1])
    alpha = gamma / delta
    one = zero - alpha * other
    resid = rhs - alpha * scaled
    partial = jnp.stack([inner(resid, one), inner(one, apply(one))])
    partial = jnp.sum(copies(partial, PLANE), axis=0)
    partial = jnp.sum(copies(partial, DEPTH), axis=0)
    newer, delta = (partial[0], partial[1])
    beta = newer / gamma
    step = newer / (delta - beta * newer / alpha)
    result = (alpha + step * beta) * zero + step * one
    return result.T[None, None]


def solution(mesh):
    finer = Mesh(mesh.devices.reshape(16, 2, 4, 4), ("gx_0", "gx_1", "gy_0", "gy_1"))
    return jax.shard_map(
        body,
        mesh=finer,
        in_specs=(
            P(GX, GY, None, None),
            P(GX, GY, None, None),
            P(GX, GY, None, None),
            P(GX, GY, None, None),
            P(GX, None, None),
            P(),
            P(GX, GY),
        ),
        out_specs=P(GX, GY, None, None),
        check_vma=False,
    )
```

time: 331 us -> 236 us (0.71)
  blocking collectives: 106 us -> 24.9 us
  waiting for transfers between devices: 72.9 us -> 57.2 us
  matrix products: 24.9 us -> 13.8 us
  other arithmetic: 12 us -> 19 us
  starting transfers between devices: 90.1 us -> 95.5 us
    psum x8 -> x0, blocking collectives: 95.4 us -> none  [by_axis(): return functools.reduce(lax.psum, axes, value)]
    all_to_all x1 -> x2, blocking collectives: 10.1 us -> 24.9 us  [exchange(): return lax.all_to_all(parts, axis, split_axis=0, concat_axis=0, tiled=True)]
    dot_general x16 -> x12, matrix products: 24.9 us -> 13.8 us  [the longest x6 9.69 us: times(): lax.dot_general(left, right, (((1,), (0,)), ((), ())), preferred_element_...]
    all_to_all x4 -> x6, waiting for transfers between devices: 56.9 us -> 48.3 us  [exchange(): return lax.all_to_all(parts, axis, split_axis=0, concat_axis=0, tiled=True)]
    ppermute x20 -> x16, waiting for transfers between devices: 16.1 us -> 8.87 us  [from_behind(): lax.ppermute(value, axis, [(source, source + steps) for source in range(f...]
    unnamed x81 -> x87, local copies, waits for them, and re-layouts: 3.08 us -> 9.78 us
    all_to_all x1 -> x6, other arithmetic: 1.07 us -> 5.32 us  [exchange(): return lax.all_to_all(parts, axis, split_axis=0, concat_axis=0, tiled=True)]
    all_to_all x4 -> x6, starting transfers between devices: 40.1 us -> 43.3 us  [exchange(): return lax.all_to_all(parts, axis, split_axis=0, concat_axis=0, tiled=True)]
  transfers between devices with their start and end apart: 24 -> 22, of which waited for: 11 -> 12; matrix products, arithmetic and copies ran while one was open for 5% -> 5% of each run, Pallas kernels for 0% -> 0%
where the time goes in v1:
time: 236 us; the launch traced here: 234 us
  starting transfers between devices  95.5 us (40%)
  waiting for transfers between devices  57.2 us (24%)
  blocking collectives  24.9 us (11%)
  local copies, waits for them, and re-layouts  22 us (9%)
  other arithmetic  19 us (8%)
  matrix products  13.8 us (6%)
    ppermute x16, starting transfers between devices, from_behind(): lax.ppermute(value, axis, [(source, source + steps) for source in range(f...  52.2 us
    all_to_all x6, waiting for transfers between devices, exchange(): return lax.all_to_all(parts, axis, split_axis=0, concat_axis=0, tiled=True)  48.3 us
    all_to_all x6, starting transfers between devices, exchange(): return lax.all_to_all(parts, axis, split_axis=0, concat_axis=0, tiled=True)  43.3 us
    all_to_all x2, blocking collectives, exchange(): return lax.all_to_all(parts, axis, split_axis=0, concat_axis=0, tiled=True)  24.9 us
    unnamed x87, local copies, waits for them, and re-layouts  9.78 us
    dot_general x6, matrix products, times(): lax.dot_general(left, right, (((1,), (0,)), ((), ())), preferred_element_...  9.69 us
    ppermute x16, waiting for transfers between devices, from_behind(): lax.ppermute(value, axis, [(source, source + steps) for source in range(f...  8.87 us
    all_to_all x6, other arithmetic, exchange(): return lax.all_to_all(parts, axis, split_axis=0, concat_axis=0, tiled=True)  5.32 us
  transfers between devices with their start and end apart: 22, of which 12 were waited for; matrix products, arithmetic and copies ran while one was open for 5% of the time, Pallas kernels for 0%

profile of v1, /device:TPU:1, one launch (start us, length us, event | category | flops | bytes accessed | tf_op | source)
XLA Modules:
  0.0 234.1 jit_solution(13920865512561076727)
XLA Ops:
  0.0 1.4 bitcast_convert_fusion
  1.6 4.9 %collective-permute-start = (bf16[192,320]{0,1:T(8,128)(2,1)S(1)}, bf16[192,320]{0,1:T(8,128)(2,1)S(1)}, u32[]{:S(2)}, u32[]{:S(2)}) collective-permute-start(bf16[192,320]{0,1:T(8,128)(2,1)S(1)} %get-tuple-element.43), channel_id=1, source_target_pairs={{0,16},{16,32},{32,48},{48,64},{64,80},{80,96},{96,112},{112,128},... | collective-permute-start | bytes 368648 | tf_op jit(solution)/shard_map/ppermute | solution.py:19
  6.5 1.3 collective-permute-start.3
  7.8 4.0 %collective-permute-start.2 = (bf16[192,320]{0,1:T(8,128)(2,1)S(1)}, bf16[192,320]{0,1:T(8,128)(2,1)S(1)}, u32[]{:S(2)}, u32[]{:S(2)}) collective-permute-start(bf16[192,320]{0,1:T(8,128)(2,1)S(1)} %get-tuple-element.45), channel_id=1, source_target_pairs={{0,1},{1,2},{2,3},{3,4},{4,5},{5,6},{6,7},{7,8},{8,9},{9,10},{10,1... | collective-permute-start | bytes 368648 | tf_op jit(solution)/shard_map/ppermute | solution.py:19
  11.8 5.7 %collective-permute-start.1 = (bf16[192,320]{0,1:T(8,128)(2,1)S(1)}, bf16[192,320]{0,1:T(8,128)(2,1)S(1)}, u32[]{:S(2)}, u32[]{:S(2)}) collective-permute-start(bf16[192,320]{0,1:T(8,128)(2,1)S(1)} %get-tuple-element.46), channel_id=1, source_target_pairs={{16,0},{32,16},{48,32},{64,48},{80,64},{96,80},{112,96},{128,112},... | collective-permute-start | bytes 368648 | tf_op jit(solution)/shard_map/ppermute | solution.py:19
  19.8 1.4 slice_add_fusion.15
  23.3 8.0 %all-to-all-start = ((f32[16,1,320]{2,1,0:T(1,128)}), f32[16,1,320]{2,1,0:T(1,128)S(1)}, u32[]{:S(2)}, u32[]{:S(2)}) async-start(f32[16,1,320]{2,1,0:T(1,128)} %reshape.118), calls=%async_computation | async-start | bytes 49152 | tf_op jit(solution)/shard_map/all_to_all | solution.py:23
  31.8 5.8 %all-to-all-done = f32[16,1,320]{2,1,0:T(1,128)S(1)} async-done(((f32[16,1,320]{2,1,0:T(1,128)}), f32[16,1,320]{2,1,0:T(1,128)S(1)}, u32[]{:S(2)}, u32[]{:S(2)}) %all-to-all-start) | async-done | bytes 20512 | tf_op jit(solution)/shard_map/all_to_all | solution.py:23
  40.0 16.2 %all-to-all-start.1 = ((f32[32,1,320]{2,1,0:T(1,128)}), f32[32,1,320]{2,1,0:T(1,128)S(1)}, u32[]{:S(2)}, u32[]{:S(2)}) async-start(f32[32,1,320]{2,1,0:T(1,128)} %reshape.120), calls=%async_computation.1 | async-start | bytes 98304 | tf_op jit(solution)/shard_map/all_to_all | solution.py:23
  56.6 12.0 %all-to-all-done.1 = f32[32,1,320]{2,1,0:T(1,128)S(1)} async-done(((f32[32,1,320]{2,1,0:T(1,128)}), f32[32,1,320]{2,1,0:T(1,128)S(1)}, u32[]{:S(2)}, u32[]{:S(2)}) %all-to-all-start.1) | async-done | bytes 40992 | tf_op jit(solution)/shard_map/all_to_all | solution.py:23
  71.3 4.1 %all-to-all-start.2 = ((f32[16,1,320]{2,1,0:T(1,128)}), f32[16,1,320]{2,1,0:T(1,128)}, u32[]{:S(2)}, u32[]{:S(2)}) async-start(f32[16,1,320]{2,1,0:T(1,128)} %reshape.122), calls=%async_computation.2 | async-start | bytes 49152 | tf_op jit(solution)/shard_map/all_to_all | solution.py:23
  75.5 1.9 convolution_bitcast_fusion.3
  77.4 4.5 %all-to-all-done.2 = f32[16,1,320]{2,1,0:T(1,128)} async-done(((f32[16,1,320]{2,1,0:T(1,128)}), f32[16,1,320]{2,1,0:T(1,128)}, u32[]{:S(2)}, u32[]{:S(2)}) %all-to-all-start.2) | async-done | bytes 20512 | tf_op jit(solution)/shard_map/all_to_all | solution.py:23
  81.9 1.5 reduce.18
  84.9 4.6 %collective-permute-start.4 = (bf16[192,320]{0,1:T(8,128)(2,1)S(1)}, bf16[192,320]{0,1:T(8,128)(2,1)S(1)}, u32[]{:S(2)}, u32[]{:S(2)}) collective-permute-start(bf16[192,320]{0,1:T(8,128)(2,1)S(1)} %get-tuple-element.39), channel_id=1, source_target_pairs={{0,16},{16,32},{32,48},{48,64},{64,80},{80,96},{96,112},{112,128},... | collective-permute-start | bytes 368648 | tf_op jit(solution)/shard_map/ppermute | solution.py:19
  89.5 1.3 collective-permute-start.7
  90.8 4.0 %collective-permute-start.6 = (bf16[192,320]{0,1:T(8,128)(2,1)S(1)}, bf16[192,320]{0,1:T(8,128)(2,1)S(1)}, u32[]{:S(2)}, u32[]{:S(2)}) collective-permute-start(bf16[192,320]{0,1:T(8,128)(2,1)S(1)} %get-tuple-element.41), channel_id=1, source_target_pairs={{0,1},{1,2},{2,3},{3,4},{4,5},{5,6},{6,7},{7,8},{8,9},{9,10},{10,1... | collective-permute-start | bytes 368648 | tf_op jit(solution)/shard_map/ppermute | solution.py:19
  94.8 1.9 collective-permute-start.5
  97.0 1.8 collective-permute-done.6
  98.8 2.6 %collective-permute-done.5 = bf16[192,320]{0,1:T(8,128)(2,1)S(1)} collective-permute-done((bf16[192,320]{0,1:T(8,128)(2,1)S(1)}, bf16[192,320]{0,1:T(8,128)(2,1)S(1)}, u32[]{:S(2)}, u32[]{:S(2)}) %collective-permute-start.5) | collective-permute-done | bytes 122912 | tf_op jit(solution)/shard_map/ppermute | solution.py:19
  102.7 1.5 multiply_reduce_fusion.2
  105.2 1.9 collective-permute-start.8
  107.1 1.3 collective-permute-start.11
  108.4 4.6 %collective-permute-start.10 = (bf16[192,320]{0,1:T(8,128)(2,1)}, bf16[192,320]{0,1:T(8,128)(2,1)}, u32[]{:S(2)}, u32[]{:S(2)}) collective-permute-start(bf16[192,320]{0,1:T(8,128)(2,1)} %get-tuple-element.37), channel_id=1, source_target_pairs={{0,1},{1,2},{2,3},{3,4},{4,5},{5,6},{6,7},{7,8},{8,9},{9,10},{10,1... | collective-permute-start | bytes 368648 | tf_op jit(solution)/shard_map/ppermute | solution.py:19
  113.0 3.6 %collective-permute-start.9 = (bf16[192,320]{0,1:T(8,128)(2,1)}, bf16[192,320]{0,1:T(8,128)(2,1)}, u32[]{:S(2)}, u32[]{:S(2)}) collective-permute-start(bf16[192,320]{0,1:T(8,128)(2,1)} %get-tuple-element.38), channel_id=1, source_target_pairs={{16,0},{32,16},{48,32},{64,48},{80,64},{96,80},{112,96},{128,112},... | collective-permute-start | bytes 368648 | tf_op jit(solution)/shard_map/ppermute | solution.py:19
  116.6 1.4 concatenate.47
  118.0 1.4 concatenate.48
  120.0 1.4 slice_add_fusion.7
  123.6 12.9 %all_to_all.40 = f32[16,1,360]{2,1,0:T(1,128)S(1)} all-to-all(f32[16,1,360]{2,1,0:T(1,128)S(1)} %reshape.124), channel_id=1, replica_groups=mesh['gx_0'=16,'gx_1'=2,'gy_0'=4,'gy_1'=4] {'gy_0','gy_1'}, dimensions={0} | all-to-all | bytes 46080 | tf_op jit(solution)/shard_map/all_to_all | solution.py:23
  138.4 6.5 %all-to-all-start.4 = ((f32[32,1,360]{2,1,0:T(1,128)}), f32[32,1,360]{2,1,0:T(1,128)S(1)}, u32[]{:S(2)}, u32[]{:S(2)}) async-start(f32[32,1,360]{2,1,0:T(1,128)} %reshape.126), calls=%async_computation.4 | async-start | bytes 98304 | tf_op jit(solution)/shard_map/all_to_all | solution.py:23
  145.9 11.4 %all-to-all-done.4 = f32[32,1,360]{2,1,0:T(1,128)S(1)} async-done(((f32[32,1,360]{2,1,0:T(1,128)}), f32[32,1,360]{2,1,0:T(1,128)S(1)}, u32[]{:S(2)}, u32[]{:S(2)}) %all-to-all-start.4) | async-done | bytes 46112 | tf_op jit(solution)/shard_map/all_to_all | solution.py:23
  159.1 1.4 copy.55
  161.2 1.2 reshape.98
  165.5 1.7 reshape.128
  167.2 3.6 %all-to-all-start.5 = ((f32[16,1,360]{2,1,0:T(1,128)}), f32[16,1,360]{2,1,0:T(1,128)S(1)}, u32[]{:S(2)}, u32[]{:S(2)}) async-start(f32[16,1,360]{2,1,0:T(1,128)} %reshape.128), calls=%async_computation.5 | async-start | bytes 49152 | tf_op jit(solution)/shard_map/all_to_all | solution.py:23
  170.9 3.0 %convolution_bitcast_fusion.1 = f32[768,320]{0,1:T(8,128)} fusion(bf16[1,1,768,768]{3,2,1,0:T(8,128)(2,1)} %param.9, f32[192,320]{0,1:T(8,128)S(1)} %copy-done.18, f32[192,320]{0,1:T(8,128)S(1)} %copy-done.21, f32[192,320]{0,1:T(8,128)} %copy-done.23, f32[192,320]{0,1:T(8,128)S(1)} %copy-done.15, f32[768]{0:T(1024)S(1)} %mul.94), kind=kOutput, calls=%fused_computation.4 | convolution fusion | flops 378716160 | bytes 3148800 | tf_op jit(solution)/shard_map/dot_general | solution.py:48
  173.8 3.2 %all-to-all-done.5 = f32[16,1,360]{2,1,0:T(1,128)S(1)} async-done(((f32[16,1,360]{2,1,0:T(1,128)}), f32[16,1,360]{2,1,0:T(1,128)S(1)}, u32[]{:S(2)}, u32[]{:S(2)}) %all-to-all-start.5) | async-done | bytes 23072 | tf_op jit(solution)/shard_map/all_to_all | solution.py:23
  178.6 1.5 fusion.53
  181.1 4.7 %collective-permute-start.12 = (bf16[192,320]{0,1:T(8,128)(2,1)}, bf16[192,320]{0,1:T(8,128)(2,1)}, u32[]{:S(2)}, u32[]{:S(2)}) collective-permute-start(bf16[192,320]{0,1:T(8,128)(2,1)} %get-tuple-element.31), channel_id=1, source_target_pairs={{0,16},{16,32},{32,48},{48,64},{64,80},{80,96},{96,112},{112,128},... | collective-permute-start | bytes 368648 | tf_op jit(solution)/shard_map/ppermute | solution.py:19
  185.9 1.3 collective-permute-start.15
  187.2 4.7 %collective-permute-start.14 = (bf16[192,320]{0,1:T(8,128)(2,1)}, bf16[192,320]{0,1:T(8,128)(2,1)}, u32[]{:S(2)}, u32[]{:S(2)}) collective-permute-start(bf16[192,320]{0,1:T(8,128)(2,1)} %get-tuple-element.33), channel_id=1, source_target_pairs={{0,1},{1,2},{2,3},{3,4},{4,5},{5,6},{6,7},{7,8},{8,9},{9,10},{10,1... | collective-permute-start | bytes 368648 | tf_op jit(solution)/shard_map/ppermute | solution.py:19
  191.8 2.3 collective-permute-start.13
  195.3 3.5 %collective-permute-done.13 = bf16[192,320]{0,1:T(8,128)(2,1)} collective-permute-done((bf16[192,320]{0,1:T(8,128)(2,1)}, bf16[192,320]{0,1:T(8,128)(2,1)}, u32[]{:S(2)}, u32[]{:S(2)}) %collective-permute-start.13) | collective-permute-done | bytes 122912 | tf_op jit(solution)/shard_map/ppermute | solution.py:19
  198.8 1.6 slice_add_fusion.3
  202.7 12.0 %all_to_all.41 = f32[32,2,320]{2,1,0:T(2,128)} all-to-all(f32[32,2,320]{2,1,0:T(2,128)S(1)} %broadcast_in_dim.37), channel_id=1, replica_groups=mesh['gx_0'=16,'gx_1'=2,'gy_0'=4,'gy_1'=4] {'gx_1','gy_0','gy_1'}, dimensions={0} | all-to-all | bytes 163840 | tf_op jit(solution)/shard_map/all_to_all | solution.py:23
  216.3 4.9 %all-to-all-start.7 = ((f32[16,2,320]{2,1,0:T(2,128)}), f32[16,2,320]{2,1,0:T(2,128)S(1)}, u32[]{:S(2)}, u32[]{:S(2)}) async-start(f32[16,2,320]{2,1,0:T(2,128)} %broadcast_in_dim.38), calls=%async_computation.7 | async-start | bytes 98304 | tf_op jit(solution)/shard_map/all_to_all | solution.py:23
  221.3 11.4 %all-to-all-done.7 = f32[16,2,320]{2,1,0:T(2,128)S(1)} async-done(((f32[16,2,320]{2,1,0:T(2,128)}), f32[16,2,320]{2,1,0:T(2,128)S(1)}, u32[]{:S(2)}, u32[]{:S(2)}) %all-to-all-start.7) | async-done | bytes 40992 | tf_op jit(solution)/shard_map/all_to_all | solution.py:23
  232.8 1.3 add_bitcast_fusion
  (163 shorter events, 32.3 us)
Async XLA Ops:
  0.0 101.7 %copy-start = (bf16[1,1,768,768]{3,2,1,0:T(8,128)(2,1)S(1)}, bf16[1,1,768,768]{3,2,1,0:T(8,128)(2,1)}, u32[]{:S(2)}) copy-start(bf16[1,1,768,768]{3,2,1,0:T(8,128)(2,1)} %param.8) | copy-start | bytes 3538948
  0.0 19.8 %copy-start.1 = (f32[1,1,320,768]{3,2,1,0:T(8,128)S(1)}, f32[1,1,320,768]{3,2,1,0:T(8,128)}, u32[]{:S(2)}) copy-start(f32[1,1,320,768]{3,2,1,0:T(8,128)} %param.7) | copy-start | bytes 2949124
  1.6 16.8 %collective-permute-start = (bf16[192,320]{0,1:T(8,128)(2,1)S(1)}, bf16[192,320]{0,1:T(8,128)(2,1)S(1)}, u32[]{:S(2)}, u32[]{:S(2)}) collective-permute-start(bf16[192,320]{0,1:T(8,128)(2,1)S(1)} %get-tuple-element.43), channel_id=1, source_target_pairs={{0,16},{16,32},{32,48},{48,64},{64,80},{80,96},{96,112},{112,128},... | collective-permute-start | bytes 368648 | tf_op jit(solution)/shard_map/ppermute | solution.py:19
  6.5 11.9 %collective-permute-start.3 = (bf16[192,320]{0,1:T(8,128)(2,1)S(1)}, bf16[192,320]{0,1:T(8,128)(2,1)S(1)}, u32[]{:S(2)}, u32[]{:S(2)}) collective-permute-start(bf16[192,320]{0,1:T(8,128)(2,1)S(1)} %get-tuple-element.44), channel_id=1, source_target_pairs={{1,0},{2,1},{3,2},{4,3},{5,4},{6,5},{7,6},{8,7},{9,8},{10,9},{11,1... | collective-permute-start | bytes 368648 | tf_op jit(solution)/shard_map/ppermute | solution.py:19
  7.8 10.6 %collective-permute-start.2 = (bf16[192,320]{0,1:T(8,128)(2,1)S(1)}, bf16[192,320]{0,1:T(8,128)(2,1)S(1)}, u32[]{:S(2)}, u32[]{:S(2)}) collective-permute-start(bf16[192,320]{0,1:T(8,128)(2,1)S(1)} %get-tuple-element.45), channel_id=1, source_target_pairs={{0,1},{1,2},{2,3},{3,4},{4,5},{5,6},{6,7},{7,8},{8,9},{9,10},{10,1... | collective-permute-start | bytes 368648 | tf_op jit(solution)/shard_map/ppermute | solution.py:19
  11.8 6.7 %collective-permute-start.1 = (bf16[192,320]{0,1:T(8,128)(2,1)S(1)}, bf16[192,320]{0,1:T(8,128)(2,1)S(1)}, u32[]{:S(2)}, u32[]{:S(2)}) collective-permute-start(bf16[192,320]{0,1:T(8,128)(2,1)S(1)} %get-tuple-element.46), channel_id=1, source_target_pairs={{16,0},{32,16},{48,32},{64,48},{80,64},{96,80},{112,96},{128,112},... | collective-permute-start | bytes 368648 | tf_op jit(solution)/shard_map/ppermute | solution.py:19
  21.3 54.2 %copy-start.2 = (f32[192,320]{0,1:T(8,128)}, f32[192,320]{0,1:T(8,128)S(1)}, u32[]{:S(2)}) copy-start(f32[192,320]{0,1:T(8,128)S(1)} %get-tuple-element.27) | copy-start | bytes 737284
  21.3 54.2 %copy-start.5 = (f32[192,320]{0,1:T(8,128)}, f32[192,320]{0,1:T(8,128)S(1)}, u32[]{:S(2)}) copy-start(f32[192,320]{0,1:T(8,128)S(1)} %get-tuple-element.28) | copy-start | bytes 737284
  21.3 54.2 %copy-start.8 = (f32[192,320]{0,1:T(8,128)}, f32[192,320]{0,1:T(8,128)S(1)}, u32[]{:S(2)}) copy-start(f32[192,320]{0,1:T(8,128)S(1)} %get-tuple-element.29) | copy-start | bytes 737284
  21.3 54.2 %copy-start.11 = (f32[192,320]{0,1:T(8,128)}, f32[192,320]{0,1:T(8,128)S(1)}, u32[]{:S(2)}) copy-start(f32[192,320]{0,1:T(8,128)S(1)} %get-tuple-element.30) | copy-start | bytes 737284
  21.3 9.9 %copy-start.35 = (f32[1,1,8,768]{3,2,1,0:T(8,128)S(1)}, f32[1,1,8,768]{3,2,1,0:T(8,128)}, u32[]{:S(2)}) copy-start(f32[1,1,8,768]{3,2,1,0:T(8,128)} %param.10) | copy-start | bytes 73732
  22.3 34.0 %copy-start.26 = (f32[1,128,128]{2,1,0:T(8,128)S(1)}, f32[1,128,128]{2,1,0:T(8,128)}, u32[]{:S(2)}) copy-start(f32[1,128,128]{2,1,0:T(8,128)} %param.11) | copy-start | bytes 196612
  23.3 14.4 %all-to-all-start = ((f32[16,1,320]{2,1,0:T(1,128)}), f32[16,1,320]{2,1,0:T(1,128)S(1)}, u32[]{:S(2)}, u32[]{:S(2)}) async-start(f32[16,1,320]{2,1,0:T(1,128)} %reshape.118), calls=%async_computation | async-start | bytes 49152 | tf_op jit(solution)/shard_map/all_to_all | solution.py:23
  40.0 28.6 %all-to-all-start.1 = ((f32[32,1,320]{2,1,0:T(1,128)}), f32[32,1,320]{2,1,0:T(1,128)S(1)}, u32[]{:S(2)}, u32[]{:S(2)}) async-start(f32[32,1,320]{2,1,0:T(1,128)} %reshape.120), calls=%async_computation.1 | async-start | bytes 98304 | tf_op jit(solution)/shard_map/all_to_all | solution.py:23
  71.3 10.6 %all-to-all-start.2 = ((f32[16,1,320]{2,1,0:T(1,128)}), f32[16,1,320]{2,1,0:T(1,128)}, u32[]{:S(2)}, u32[]{:S(2)}) async-start(f32[16,1,320]{2,1,0:T(1,128)} %reshape.122), calls=%async_computation.2 | async-start | bytes 49152 | tf_op jit(solution)/shard_map/all_to_all | solution.py:23
  84.9 11.8 %collective-permute-start.4 = (bf16[192,320]{0,1:T(8,128)(2,1)S(1)}, bf16[192,320]{0,1:T(8,128)(2,1)S(1)}, u32[]{:S(2)}, u32[]{:S(2)}) collective-permute-start(bf16[192,320]{0,1:T(8,128)(2,1)S(1)} %get-tuple-element.39), channel_id=1, source_target_pairs={{0,16},{16,32},{32,48},{48,64},{64,80},{80,96},{96,112},{112,128},... | collective-permute-start | bytes 368648 | tf_op jit(solution)/shard_map/ppermute | solution.py:19
  89.5 7.5 %collective-permute-start.7 = (bf16[192,320]{0,1:T(8,128)(2,1)S(1)}, bf16[192,320]{0,1:T(8,128)(2,1)S(1)}, u32[]{:S(2)}, u32[]{:S(2)}) collective-permute-start(bf16[192,320]{0,1:T(8,128)(2,1)S(1)} %get-tuple-element.40), channel_id=1, source_target_pairs={{1,0},{2,1},{3,2},{4,3},{5,4},{6,5},{7,6},{8,7},{9,8},{10,9},{11,1... | collective-permute-start | bytes 368648 | tf_op jit(solution)/shard_map/ppermute | solution.py:19
  90.8 8.0 %collective-permute-start.6 = (bf16[192,320]{0,1:T(8,128)(2,1)S(1)}, bf16[192,320]{0,1:T(8,128)(2,1)S(1)}, u32[]{:S(2)}, u32[]{:S(2)}) collective-permute-start(bf16[192,320]{0,1:T(8,128)(2,1)S(1)} %get-tuple-element.41), channel_id=1, source_target_pairs={{0,1},{1,2},{2,3},{3,4},{4,5},{5,6},{6,7},{7,8},{8,9},{9,10},{10,1... | collective-permute-start | bytes 368648 | tf_op jit(solution)/shard_map/ppermute | solution.py:19
  94.8 6.6 %collective-permute-start.5 = (bf16[192,320]{0,1:T(8,128)(2,1)S(1)}, bf16[192,320]{0,1:T(8,128)(2,1)S(1)}, u32[]{:S(2)}, u32[]{:S(2)}) collective-permute-start(bf16[192,320]{0,1:T(8,128)(2,1)S(1)} %get-tuple-element.42), channel_id=1, source_target_pairs={{16,0},{32,16},{48,32},{64,48},{80,64},{96,80},{112,96},{128,112},... | collective-permute-start | bytes 368648 | tf_op jit(solution)/shard_map/ppermute | solution.py:19
  105.2 14.2 %collective-permute-start.8 = (bf16[192,320]{0,1:T(8,128)(2,1)}, bf16[192,320]{0,1:T(8,128)(2,1)}, u32[]{:S(2)}, u32[]{:S(2)}) collective-permute-start(bf16[192,320]{0,1:T(8,128)(2,1)} %get-tuple-element.35), channel_id=1, source_target_pairs={{0,16},{16,32},{32,48},{48,64},{64,80},{80,96},{96,112},{112,128},... | collective-permute-start | bytes 368648 | tf_op jit(solution)/shard_map/ppermute | solution.py:19
  107.1 12.3 %collective-permute-start.11 = (bf16[192,320]{0,1:T(8,128)(2,1)}, bf16[192,320]{0,1:T(8,128)(2,1)}, u32[]{:S(2)}, u32[]{:S(2)}) collective-permute-start(bf16[192,320]{0,1:T(8,128)(2,1)} %get-tuple-element.36), channel_id=1, source_target_pairs={{1,0},{2,1},{3,2},{4,3},{5,4},{6,5},{7,6},{8,7},{9,8},{10,9},{11,1... | collective-permute-start | bytes 368648 | tf_op jit(solution)/shard_map/ppermute | solution.py:19
  108.4 11.0 %collective-permute-start.10 = (bf16[192,320]{0,1:T(8,128)(2,1)}, bf16[192,320]{0,1:T(8,128)(2,1)}, u32[]{:S(2)}, u32[]{:S(2)}) collective-permute-start(bf16[192,320]{0,1:T(8,128)(2,1)} %get-tuple-element.37), channel_id=1, source_target_pairs={{0,1},{1,2},{2,3},{3,4},{4,5},{5,6},{6,7},{7,8},{8,9},{9,10},{10,1... | collective-permute-start | bytes 368648 | tf_op jit(solution)/shard_map/ppermute | solution.py:19
  113.0 6.9 %collective-permute-start.9 = (bf16[192,320]{0,1:T(8,128)(2,1)}, bf16[192,320]{0,1:T(8,128)(2,1)}, u32[]{:S(2)}, u32[]{:S(2)}) collective-permute-start(bf16[192,320]{0,1:T(8,128)(2,1)} %get-tuple-element.38), channel_id=1, source_target_pairs={{16,0},{32,16},{48,32},{64,48},{80,64},{96,80},{112,96},{128,112},... | collective-permute-start | bytes 368648 | tf_op jit(solution)/shard_map/ppermute | solution.py:19
  120.0 2.2 copy-start.36
  121.4 1.7 copy-start.17
  121.4 1.7 copy-start.20
  121.4 1.7 copy-start.23
  121.4 2.0 copy-start.32
  121.4 2.0 copy-start.33
  138.4 18.9 %all-to-all-start.4 = ((f32[32,1,360]{2,1,0:T(1,128)}), f32[32,1,360]{2,1,0:T(1,128)S(1)}, u32[]{:S(2)}, u32[]{:S(2)}) async-start(f32[32,1,360]{2,1,0:T(1,128)} %reshape.126), calls=%async_computation.4 | async-start | bytes 98304 | tf_op jit(solution)/shard_map/all_to_all | solution.py:23
  158.3 12.5 %copy-start.15 = (f32[192,320]{0,1:T(8,128)S(1)}, f32[192,320]{0,1:T(8,128)}, u32[]{:S(2)}) copy-start(f32[192,320]{0,1:T(8,128)} %copy-done.14) | copy-start | bytes 737284
  158.3 12.5 %copy-start.18 = (f32[192,320]{0,1:T(8,128)S(1)}, f32[192,320]{0,1:T(8,128)}, u32[]{:S(2)}) copy-start(f32[192,320]{0,1:T(8,128)} %copy-done.17) | copy-start | bytes 737284
  161.2 9.6 %copy-start.21 = (f32[192,320]{0,1:T(8,128)S(1)}, f32[192,320]{0,1:T(8,128)}, u32[]{:S(2)}) copy-start(f32[192,320]{0,1:T(8,128)} %copy-done.20) | copy-start | bytes 737284
  167.2 9.9 %all-to-all-start.5 = ((f32[16,1,360]{2,1,0:T(1,128)}), f32[16,1,360]{2,1,0:T(1,128)S(1)}, u32[]{:S(2)}, u32[]{:S(2)}) async-start(f32[16,1,360]{2,1,0:T(1,128)} %reshape.128), calls=%async_computation.5 | async-start | bytes 49152 | tf_op jit(solution)/shard_map/all_to_all | solution.py:23
  170.9 7.8 %copy-start.31 = (bf16[8,768]{1,0:T(8,128)(2,1)S(1)}, bf16[8,768]{1,0:T(8,128)(2,1)}, u32[]{:S(2)}) copy-start(bf16[8,768]{1,0:T(8,128)(2,1)} %get-tuple-element.48) | copy-start | bytes 36868
  181.1 14.1 %collective-permute-start.12 = (bf16[192,320]{0,1:T(8,128)(2,1)}, bf16[192,320]{0,1:T(8,128)(2,1)}, u32[]{:S(2)}, u32[]{:S(2)}) collective-permute-start(bf16[192,320]{0,1:T(8,128)(2,1)} %get-tuple-element.31), channel_id=1, source_target_pairs={{0,16},{16,32},{32,48},{48,64},{64,80},{80,96},{96,112},{112,128},... | collective-permute-start | bytes 368648 | tf_op jit(solution)/shard_map/ppermute | solution.py:19
  185.9 9.4 %collective-permute-start.15 = (bf16[192,320]{0,1:T(8,128)(2,1)}, bf16[192,320]{0,1:T(8,128)(2,1)}, u32[]{:S(2)}, u32[]{:S(2)}) collective-permute-start(bf16[192,320]{0,1:T(8,128)(2,1)} %get-tuple-element.32), channel_id=1, source_target_pairs={{1,0},{2,1},{3,2},{4,3},{5,4},{6,5},{7,6},{8,7},{9,8},{10,9},{11,1... | collective-permute-start | bytes 368648 | tf_op jit(solution)/shard_map/ppermute | solution.py:19
  187.2 8.1 %collective-permute-start.14 = (bf16[192,320]{0,1:T(8,128)(2,1)}, bf16[192,320]{0,1:T(8,128)(2,1)}, u32[]{:S(2)}, u32[]{:S(2)}) collective-permute-start(bf16[192,320]{0,1:T(8,128)(2,1)} %get-tuple-element.33), channel_id=1, source_target_pairs={{0,1},{1,2},{2,3},{3,4},{4,5},{5,6},{6,7},{7,8},{8,9},{9,10},{10,1... | collective-permute-start | bytes 368648 | tf_op jit(solution)/shard_map/ppermute | solution.py:19
  191.8 6.9 %collective-permute-start.13 = (bf16[192,320]{0,1:T(8,128)(2,1)}, bf16[192,320]{0,1:T(8,128)(2,1)}, u32[]{:S(2)}, u32[]{:S(2)}) collective-permute-start(bf16[192,320]{0,1:T(8,128)(2,1)} %get-tuple-element.34), channel_id=1, source_target_pairs={{16,0},{32,16},{48,32},{64,48},{80,64},{96,80},{112,96},{128,112},... | collective-permute-start | bytes 368648 | tf_op jit(solution)/shard_map/ppermute | solution.py:19
  198.8 1.6 copy-start.4
  198.8 1.6 copy-start.7
  198.8 1.6 copy-start.10
  198.8 1.6 copy-start.13
  198.8 1.7 copy-start.16
  198.8 1.8 copy-start.19
  198.8 1.9 copy-start.22
  198.8 1.9 copy-start.24
  216.3 16.4 %all-to-all-start.7 = ((f32[16,2,320]{2,1,0:T(2,128)}), f32[16,2,320]{2,1,0:T(2,128)S(1)}, u32[]{:S(2)}, u32[]{:S(2)}) async-start(f32[16,2,320]{2,1,0:T(2,128)} %broadcast_in_dim.38), calls=%async_computation.7 | async-start | bytes 98304 | tf_op jit(solution)/shard_map/all_to_all | solution.py:23
  (11 other events, 10.1 us)

commit v2 on v1

v2 whole, which is shorter than its diff:
```python
import jax
import jax.numpy as jnp
from jax import lax
from jax.sharding import Mesh
from jax.sharding import PartitionSpec as P

NAGG = 2
GX = ("gx_0", "gx_1")
GY = ("gy_0", "gy_1")
CORE = ("gx_1",)
PLANE = ("gx_1", "gy_0", "gy_1")
DEPTH = ("gx_0",)

HIGH = lax.Precision.HIGHEST


def traded(value, axis, first):
    count = lax.axis_size(axis)
    pairs = [(k, k + 1) for k in range(first, count - 1, 2)]
    return lax.ppermute(value, axis, pairs + [(b, a) for a, b in pairs])


def copies(value, axis):
    parts = jnp.broadcast_to(value, (lax.axis_size(axis), *value.shape))
    return lax.all_to_all(parts, axis, split_axis=0, concat_axis=0, tiled=True)


def edges_of(vec):
    width = vec.shape[0] // 4
    return [vec[k * width : (k + 1) * width] for k in range(4)]


def neighbours(parts):
    west, east, south, north = parts
    left = lax.axis_index(GX) % 2 == 0
    lower = lax.axis_index(GY) % 2 == 0
    far_y = traded(jnp.where(lower, south, north), GY, 1)
    near_y = traded(jnp.where(lower, north, south), GY, 0)
    far_x = traded(jnp.where(left, west, east), GX, 1)
    near_x = traded(jnp.where(left, east, west), GX, 0)
    return (
        jnp.where(left, far_x, near_x),
        jnp.where(left, near_x, far_x),
        jnp.where(lower, far_y, near_y),
        jnp.where(lower, near_y, far_y),
    )


def assemble(vec):
    others = neighbours(edges_of(vec.astype(jnp.bfloat16)))
    return jnp.concatenate(
        [mine + other.astype(vec.dtype) for mine, other in zip(edges_of(vec), others)], axis=0
    )


def halves(value):
    upper = lax.reduce_precision(value, 8, 7)
    return (upper.astype(jnp.bfloat16), (value - upper).astype(jnp.bfloat16))


def times(left, right):
    return lax.dot_general(
        left, right, (((1,), (0,)), ((), ())), preferred_element_type=jnp.float32
    )


def times_high(left, right):
    return lax.dot_general(
        left,
        right,
        (((1,), (0,)), ((), ())),
        precision=HIGH,
        preferred_element_type=jnp.float32,
    )


def body(load, stiffness, local_inverse, phi, level2_inverse, level3_inverse, aggregate):
    load_here = load[0, 0].T
    stiff = stiffness[0, 0]
    inverse = local_inverse[0, 0]
    basis = phi[0, 0]
    total, rows = load_here.shape
    width = total // 4
    count = basis.shape[0]
    block = NAGG * count
    col = lax.axis_index(GX)
    row = lax.axis_index(GY)
    core = lax.axis_index(CORE)
    cols_total = lax.axis_size(GX)
    rows_total = lax.axis_size(GY)
    cores = lax.axis_size(CORE)
    edge_w = jnp.stack(
        [
            jnp.where(col > 0, 0.5, 1.0),
            jnp.where(col < cols_total - 1, 0.5, 1.0),
            jnp.where(row > 0, 0.5, 1.0),
            jnp.where(row < rows_total - 1, 0.5, 1.0),
        ]
    ).astype(jnp.float32)
    weights = jnp.repeat(edge_w, width)[:, None]
    own = aggregate[0, 0]
    second_inv = lax.dynamic_slice_in_dim(level2_inverse[0], row * count, count, 0)
    third_inv = lax.dynamic_slice_in_dim(
        level3_inverse, (col - core) * block, cores * block, 0
    )
    third_inv = third_inv.reshape(cores * block, cols_total // cores, cores, block)
    third_inv = lax.dynamic_index_in_dim(third_inv, core, 2, keepdims=False)
    planes = cols_total // cores
    third_first = third_inv.reshape(cores * block, planes * block)
    adders = jnp.array([[1, 0, 1, 0, 0, 0, 0, 0], [0, 1, 0, 1, 0, 0, 0, 0]], jnp.bfloat16)
    adders = jnp.pad(adders, ((0, 6), (block, 0)))
    third_dots = jnp.concatenate(
        [
            jnp.pad(third_inv, ((0, 0), (0, 0), (0, 8))),
            jnp.broadcast_to(adders[:, None], (8, planes, block + 8)),
        ],
        axis=0,
    ).reshape(-1, planes * (block + 8))
    basis_hi, basis_lo = halves(basis)
    spread = jnp.concatenate([basis_hi, basis_lo, basis_hi], axis=0).T
    tags = jnp.broadcast_to(own.astype(jnp.float32), (count, 128 - rows % 128))

    def swapped(value):
        return lax.ppermute(value, CORE, [(0, 1), (1, 0)])

    def precondition(scaled, extra, members):
        primal = times_high(basis, scaled)
        local = times(inverse, scaled.astype(jnp.bfloat16))
        if members is None:
            group = copies(jnp.concatenate([primal, tags], axis=1), GY)
            members = group[:, :1, rows : rows + 1]
            group = group[:, :, :rows]
        else:
            group = copies(jnp.concatenate([primal, extra], axis=0), GY)
        group, found = (group[:, :count], group[:, count:])
        summed = [
            jnp.sum(jnp.where(members == label, group, 0.0), axis=0) for label in range(NAGG)
        ]
        third_inv = third_first
        if extra is not None:
            found = jnp.sum(found, axis=0)
            upper = lax.reduce_precision(found, 8, 7)
            at = lax.broadcasted_iota(jnp.int32, found.shape, 0)
            summed.append(jnp.where(at < 2, upper, jnp.where(at < 4, found - upper, 0.0)))
            third_inv = third_dots
        everyone = copies(jnp.concatenate(summed, axis=0).astype(jnp.bfloat16), DEPTH)
        second = times_high(second_inv, group.reshape(rows_total * count, rows))
        parts = times(third_inv, everyone.reshape(-1, rows))
        here, there = (parts[:block], parts[block : 2 * block])
        kept = jnp.where(core == 0, here, there)
        sent = jnp.where(core == 0, there, here)
        dots = parts[2 * block :]
        got = swapped(jnp.concatenate([sent, dots], axis=0))
        third = kept + got[:block]
        third_own = third[:count]
        for label in range(1, NAGG):
            third_own = jnp.where(own == label, third[label * count : (label + 1) * count], third_own)
        coarse_hi, coarse_lo = halves(second + third_own)
        stacked = jnp.concatenate([coarse_hi, coarse_hi, coarse_lo], axis=0)
        full = local + times(spread, stacked)
        return (assemble(weights * full), members, dots + got[block:])

    def apply(vec):
        return times(stiff, vec.astype(jnp.bfloat16))

    def inner(left, right):
        return jnp.sum(left * right, axis=0)

    rhs = weights * assemble(load_here)
    zero, members, _ = precondition(rhs, None, None)
    image = apply(zero)
    dots = jnp.stack([inner(rhs, zero), inner(zero, image)])
    dots = jnp.concatenate([dots, dots, jnp.zeros((4, rows), jnp.float32)], axis=0)
    scaled = weights * assemble(image)
    other, _, dots = precondition(scaled, dots, members)
    gamma, delta = (dots[0], dots[1])
    alpha = gamma / delta
    one = zero - alpha * other
    resid = rhs - alpha * scaled
    partial = jnp.stack([inner(resid, one), inner(one, apply(one))])
    partial = jnp.sum(copies(partial, PLANE), axis=0)
    partial = jnp.sum(copies(partial, DEPTH), axis=0)
    newer, delta = (partial[0], partial[1])
    beta = newer / gamma
    step = newer / (delta - beta * newer / alpha)
    result = (alpha + step * beta) * zero + step * one
    return result.T[None, None]


def solution(mesh):
    finer = Mesh(mesh.devices.reshape(16, 2, 4, 4), ("gx_0", "gx_1", "gy_0", "gy_1"))
    return jax.shard_map(
        body,
        mesh=finer,
        in_specs=(
            P(GX, GY, None, None),
            P(GX, GY, None, None),
            P(GX, GY, None, None),
            P(GX, GY, None, None),
            P(GX, None, None),
            P(),
            P(GX, GY),
        ),
        out_specs=P(GX, GY, None, None),
        check_vma=False,
    )
```

time: 236 us -> 207 us (0.88)
  blocking collectives: 24.9 us -> 45.2 us
  waiting for transfers between devices: 57.2 us -> 36.9 us
  local copies, waits for them, and re-layouts: 22 us -> 10.5 us
  other arithmetic: 19 us -> 10.8 us
  starting transfers between devices: 95.5 us -> 89.6 us
  matrix products: 13.8 us -> 11.4 us
    all_to_all x2 -> x3, blocking collectives: 24.9 us -> 45.2 us  [copies(): return lax.all_to_all(parts, axis, split_axis=0, concat_axis=0, tiled=True)]
    all_to_all x6 -> x3, waiting for transfers between devices: 48.3 us -> 31.7 us  [copies(): return lax.all_to_all(parts, axis, split_axis=0, concat_axis=0, tiled=True)]
    all_to_all x6 -> x3, starting transfers between devices: 43.3 us -> 28.3 us  [copies(): return lax.all_to_all(parts, axis, split_axis=0, concat_axis=0, tiled=True)]
    ppermute x16 -> x18, starting transfers between devices: 52.2 us -> 61.3 us  [the longest x16 44.2 us: traded(): return lax.ppermute(value, axis, pairs + [(b, a) for a, b in pairs])]
    all_to_all x6 -> x0, other arithmetic: 5.32 us -> none  [exchange(): return lax.all_to_all(parts, axis, split_axis=0, concat_axis=0, tiled=True)]
    unnamed x87 -> x67, local copies, waits for them, and re-layouts: 9.78 us -> 5.01 us
    ppermute x16 -> x18, waiting for transfers between devices: 8.87 us -> 5.21 us  [the longest x16 5.2 us: traded(): return lax.ppermute(value, axis, pairs + [(b, a) for a, b in pairs])]
    add x6 -> x7, other arithmetic: 5.53 us -> 2.25 us  [the longest x4 2.23 us: assemble(): mine + other.astype(vec.dtype)]
  transfers between devices with their start and end apart: 22 -> 21, of which waited for: 12 -> 10; matrix products, arithmetic and copies ran while one was open for 5% -> 4% of each run, Pallas kernels for 0% -> 0%
where the time goes in v2:
time: 207 us; the launch traced here: 206 us
  starting transfers between devices  89.6 us (43%)
  blocking collectives  45.2 us (22%)
  waiting for transfers between devices  36.9 us (18%)
  matrix products  11.4 us (6%)
  other arithmetic  10.8 us (5%)
  local copies, waits for them, and re-layouts  10.5 us (5%)
    all_to_all x3, blocking collectives, copies(): return lax.all_to_all(parts, axis, split_axis=0, concat_axis=0, tiled=True)  45.2 us
    ppermute x16, starting transfers between devices, traded(): return lax.ppermute(value, axis, pairs + [(b, a) for a, b in pairs])  44.2 us
    all_to_all x3, waiting for transfers between devices, copies(): return lax.all_to_all(parts, axis, split_axis=0, concat_axis=0, tiled=True)  31.7 us
    all_to_all x3, starting transfers between devices, copies(): return lax.all_to_all(parts, axis, split_axis=0, concat_axis=0, tiled=True)  28.3 us
    ppermute x2, starting transfers between devices, swapped(): return lax.ppermute(value, CORE, [(0, 1), (1, 0)])  17.1 us
    dot_general x8, matrix products, times(): lax.dot_general(left, right, (((1,), (0,)), ((), ())), preferred_element_...  7.7 us
    ppermute x16, waiting for transfers between devices, traded(): return lax.ppermute(value, axis, pairs + [(b, a) for a, b in pairs])  5.2 us
    unnamed x67, local copies, waits for them, and re-layouts  5.01 us
  transfers between devices with their start and end apart: 21, of which 10 were waited for; matrix products, arithmetic and copies ran while one was open for 4% of the time, Pallas kernels for 0%

profile of v2, /device:TPU:1, one launch (start us, length us, event | category | flops | bytes accessed | tf_op | source)
XLA Modules:
  0.0 205.9 jit_solution(12267853104901221790)
XLA Ops:
  0.0 1.4 bitcast_convert_fusion
  1.6 4.9 %collective-permute-start = (bf16[192,320]{0,1:T(8,128)(2,1)S(1)}, bf16[192,320]{0,1:T(8,128)(2,1)S(1)}, u32[]{:S(2)}, u32[]{:S(2)}) collective-permute-start(bf16[192,320]{0,1:T(8,128)(2,1)S(1)} %get-tuple-element.59), channel_id=1, source_target_pairs={{16,32},{48,64},{80,96},{112,128},{144,160},{176,192},{208,224},{2... | collective-permute-start | bytes 368648 | tf_op jit(solution)/shard_map/ppermute | solution.py:20
  7.2 5.7 %collective-permute-start.3 = (bf16[192,320]{0,1:T(8,128)(2,1)S(1)}, bf16[192,320]{0,1:T(8,128)(2,1)S(1)}, u32[]{:S(2)}, u32[]{:S(2)}) collective-permute-start(bf16[192,320]{0,1:T(8,128)(2,1)S(1)} %get-tuple-element.61), channel_id=1, source_target_pairs={{0,1},{2,3},{4,5},{6,7},{8,9},{10,11},{12,13},{14,15},{1,0},{3,2},... | collective-permute-start | bytes 368648 | tf_op jit(solution)/shard_map/ppermute | solution.py:20
  12.9 1.9 collective-permute-start.1
  15.8 1.2 collective-permute-done.3
  18.3 1.4 slice_add_fusion.15
  19.8 0.9 convolution_bitcast_fusion.6
  20.8 11.6 %all_to_all.30 = f32[16,8,384]{2,1,0:T(8,128)S(1)} all-to-all(f32[16,8,384]{2,1,0:T(8,128)S(1)} %broadcast_in_dim.74), channel_id=1, replica_groups=mesh['gx_0'=16,'gx_1'=2,'gy_0'=4,'gy_1'=4] {'gy_0','gy_1'}, dimensions={0} | all-to-all | bytes 393216 | tf_op jit(solution)/shard_map/all_to_all | solution.py:25
  32.5 0.7 compare_reduce_fusion.1
  34.4 15.9 %all-to-all-start.1 = ((bf16[16,16,320]{2,1,0:T(8,128)(2,1)}), bf16[16,16,320]{2,1,0:T(8,128)(2,1)S(1)}, u32[]{:S(2)}, u32[]{:S(2)}) async-start(bf16[16,16,320]{2,1,0:T(8,128)(2,1)} %broadcast_in_dim.80), calls=%async_computation.1 | async-start | bytes 393216 | tf_op jit(solution)/shard_map/all_to_all | solution.py:25
  50.4 0.8 constant_dynamic-slice_fusion.1
  51.3 11.3 %all-to-all-done.1 = bf16[16,16,320]{2,1,0:T(8,128)(2,1)S(1)} async-done(((bf16[16,16,320]{2,1,0:T(8,128)(2,1)}), bf16[16,16,320]{2,1,0:T(8,128)(2,1)S(1)}, u32[]{:S(2)}, u32[]{:S(2)}) %all-to-all-start.1) | async-done | bytes 163872 | tf_op jit(solution)/shard_map/all_to_all | solution.py:25
  62.9 7.5 %collective-permute-start.4 = (f32[16,320]{1,0:T(8,128)S(1)}, f32[16,320]{1,0:T(8,128)S(1)}, u32[]{:S(2)}, u32[]{:S(2)}) collective-permute-start(f32[16,320]{1,0:T(8,128)S(1)} %slice_select_fusion.1), channel_id=1, source_target_pairs={{0,16},{16,0},{1,17},{17,1},{2,18},{18,2},{3,19},{19,3},{4,20},{20... | collective-permute-start | bytes 61448 | tf_op jit(solution)/shard_map/ppermute | solution.py:124
  70.4 1.9 convolution_bitcast_fusion.3
  72.3 0.9 reduce-precision_convert_fusion.2
  73.7 3.2 %collective-permute-start.5 = (bf16[192,320]{0,1:T(8,128)(2,1)S(1)}, bf16[192,320]{0,1:T(8,128)(2,1)S(1)}, u32[]{:S(2)}, u32[]{:S(2)}) collective-permute-start(bf16[192,320]{0,1:T(8,128)(2,1)S(1)} %get-tuple-element.55), channel_id=1, source_target_pairs={{16,32},{48,64},{80,96},{112,128},{144,160},{176,192},{208,224},{2... | collective-permute-start | bytes 368648 | tf_op jit(solution)/shard_map/ppermute | solution.py:20
  77.6 4.2 %collective-permute-start.8 = (bf16[192,320]{0,1:T(8,128)(2,1)S(1)}, bf16[192,320]{0,1:T(8,128)(2,1)S(1)}, u32[]{:S(2)}, u32[]{:S(2)}) collective-permute-start(bf16[192,320]{0,1:T(8,128)(2,1)S(1)} %get-tuple-element.57), channel_id=1, source_target_pairs={{0,1},{2,3},{4,5},{6,7},{8,9},{10,11},{12,13},{14,15},{1,0},{3,2},... | collective-permute-start | bytes 368648 | tf_op jit(solution)/shard_map/ppermute | solution.py:20
  81.8 1.9 collective-permute-start.6
  83.7 0.7 collective-permute-done.8
  86.4 0.9 multiply_reduce_fusion.1
  87.4 3.8 %collective-permute-start.9 = (bf16[192,320]{0,1:T(8,128)(2,1)S(1)}, bf16[192,320]{0,1:T(8,128)(2,1)S(1)}, u32[]{:S(2)}, u32[]{:S(2)}) collective-permute-start(bf16[192,320]{0,1:T(8,128)(2,1)S(1)} %get-tuple-element.51), channel_id=1, source_target_pairs={{16,32},{48,64},{80,96},{112,128},{144,160},{176,192},{208,224},{2... | collective-permute-start | bytes 368648 | tf_op jit(solution)/shard_map/ppermute | solution.py:20
  91.9 5.3 %collective-permute-start.12 = (bf16[192,320]{0,1:T(8,128)(2,1)S(1)}, bf16[192,320]{0,1:T(8,128)(2,1)S(1)}, u32[]{:S(2)}, u32[]{:S(2)}) collective-permute-start(bf16[192,320]{0,1:T(8,128)(2,1)S(1)} %get-tuple-element.53), channel_id=1, source_target_pairs={{0,1},{2,3},{4,5},{6,7},{8,9},{10,11},{12,13},{14,15},{1,0},{3,2},... | collective-permute-start | bytes 368648 | tf_op jit(solution)/shard_map/ppermute | solution.py:20
  97.2 1.9 collective-permute-start.10
  99.1 0.7 collective-permute-done.12
  101.5 0.9 convolution_bitcast_fusion.5
  102.5 0.8 broadcast_in_dim.82
  103.3 5.9 %all-to-all-start.2 = ((f32[16,16,320]{2,1,0:T(8,128)}), f32[16,16,320]{2,1,0:T(8,128)S(1)}, u32[]{:S(2)}, u32[]{:S(2)}) async-start(f32[16,16,320]{2,1,0:T(8,128)} %broadcast_in_dim.82), calls=%async_computation.2 | async-start | bytes 786432 | tf_op jit(solution)/shard_map/all_to_all | solution.py:25
  109.8 8.7 %all-to-all-done.2 = f32[16,16,320]{2,1,0:T(8,128)S(1)} async-done(((f32[16,16,320]{2,1,0:T(8,128)}), f32[16,16,320]{2,1,0:T(8,128)S(1)}, u32[]{:S(2)}, u32[]{:S(2)}) %all-to-all-start.2) | async-done | bytes 327712 | tf_op jit(solution)/shard_map/all_to_all | solution.py:25
  118.5 0.7 select_reduce_fusion.1
  119.2 0.7 fusion.41
  120.0 0.7 broadcast_in_dim.84
  120.7 6.4 %all-to-all-start.3 = ((bf16[16,24,320]{2,1,0:T(8,128)(2,1)}), bf16[16,24,320]{2,1,0:T(8,128)(2,1)}, u32[]{:S(2)}, u32[]{:S(2)}) async-start(bf16[16,24,320]{2,1,0:T(8,128)(2,1)} %broadcast_in_dim.84), calls=%async_computation.3 | async-start | bytes 589824 | tf_op jit(solution)/shard_map/all_to_all | solution.py:25
  127.1 1.5 fusion.73
  128.6 11.7 %all-to-all-done.3 = bf16[16,24,320]{2,1,0:T(8,128)(2,1)} async-done(((bf16[16,24,320]{2,1,0:T(8,128)(2,1)}), bf16[16,24,320]{2,1,0:T(8,128)(2,1)}, u32[]{:S(2)}, u32[]{:S(2)}) %all-to-all-start.3) | async-done | bytes 245792 | tf_op jit(solution)/shard_map/all_to_all | solution.py:25
  140.3 0.7 broadcast_in_dim.72
  141.0 1.3 convolution_bitcast_fusion.4
  142.4 9.6 %collective-permute-start.13 = (f32[24,320]{1,0:T(8,128)S(1)}, f32[24,320]{1,0:T(8,128)S(1)}, u32[]{:S(2)}, u32[]{:S(2)}) collective-permute-start(f32[24,320]{1,0:T(8,128)S(1)} %pad_maximum_fusion.2), channel_id=1, source_target_pairs={{0,16},{16,0},{1,17},{17,1},{2,18},{18,2},{3,19},{19,3},{4,20},{20... | collective-permute-start | bytes 92168 | tf_op jit(solution)/shard_map/ppermute | solution.py:124
  152.0 2.1 %convolution_bitcast_fusion.1 = f32[768,320]{0,1:T(8,128)S(1)} fusion(bf16[1,1,768,768]{3,2,1,0:T(8,128)(2,1)} %param.10, f32[192,320]{0,1:T(8,128)} %copy-done.19, f32[192,320]{0,1:T(8,128)} %copy-done.21, f32[192,320]{0,1:T(8,128)S(1)} %get-tuple-element.27, f32[192,320]{0,1:T(8,128)S(1)} %copy-done.15, f32[768]{0:T(1024)S(1)} %mul.108), kind=kOutput, calls=%fused_computation.4 | convolution fusion | flops 378716160 | bytes 3148800 | tf_op jit(solution)/shard_map/dot_general | solution.py:62
  154.2 0.9 reduce-precision_convert_fusion.1
  155.6 2.9 %collective-permute-start.14 = (bf16[192,320]{0,1:T(8,128)(2,1)S(1)}, bf16[192,320]{0,1:T(8,128)(2,1)S(1)}, u32[]{:S(2)}, u32[]{:S(2)}) collective-permute-start(bf16[192,320]{0,1:T(8,128)(2,1)S(1)} %get-tuple-element.47), channel_id=1, source_target_pairs={{16,32},{48,64},{80,96},{112,128},{144,160},{176,192},{208,224},{2... | collective-permute-start | bytes 368648 | tf_op jit(solution)/shard_map/ppermute | solution.py:20
  159.2 3.9 %collective-permute-start.17 = (bf16[192,320]{0,1:T(8,128)(2,1)S(1)}, bf16[192,320]{0,1:T(8,128)(2,1)S(1)}, u32[]{:S(2)}, u32[]{:S(2)}) collective-permute-start(bf16[192,320]{0,1:T(8,128)(2,1)S(1)} %get-tuple-element.49), channel_id=1, source_target_pairs={{0,1},{2,3},{4,5},{6,7},{8,9},{10,11},{12,13},{14,15},{1,0},{3,2},... | collective-permute-start | bytes 368648 | tf_op jit(solution)/shard_map/ppermute | solution.py:20
  163.1 1.9 collective-permute-start.15
  165.1 1.2 collective-permute-done.17
  168.1 1.1 multiply_reduce_fusion
  170.0 14.1 %all_to_all.31 = f32[32,2,320]{2,1,0:T(2,128)} all-to-all(f32[32,2,320]{2,1,0:T(2,128)S(1)} %broadcast_in_dim.85), channel_id=1, replica_groups=mesh['gx_0'=16,'gx_1'=2,'gy_0'=4,'gy_1'=4] {'gx_1','gy_0','gy_1'}, dimensions={0} | all-to-all | bytes 163840 | tf_op jit(solution)/shard_map/all_to_all | solution.py:25
  184.1 0.9 reduce_sum.108
  185.0 19.5 %all_to_all.32 = f32[16,2,320]{2,1,0:T(2,128)S(1)} all-to-all(f32[16,2,320]{2,1,0:T(2,128)S(1)} %broadcast_in_dim.86), channel_id=1, replica_groups=mesh['gx_0'=16,'gx_1'=2,'gy_0'=4,'gy_1'=4] {'gx_0'}, dimensions={0} | all-to-all | bytes 81920 | tf_op jit(solution)/shard_map/all_to_all | solution.py:25
  204.6 1.3 add_bitcast_fusion
  (128 shorter events, 14.0 us)
Async XLA Ops:
  0.0 85.4 %copy-start = (bf16[1,1,768,768]{3,2,1,0:T(8,128)(2,1)S(1)}, bf16[1,1,768,768]{3,2,1,0:T(8,128)(2,1)}, u32[]{:S(2)}) copy-start(bf16[1,1,768,768]{3,2,1,0:T(8,128)(2,1)} %param.9) | copy-start | bytes 3538948
  0.0 18.3 %copy-start.1 = (f32[1,1,320,768]{3,2,1,0:T(8,128)S(1)}, f32[1,1,320,768]{3,2,1,0:T(8,128)}, u32[]{:S(2)}) copy-start(f32[1,1,320,768]{3,2,1,0:T(8,128)} %param.8) | copy-start | bytes 2949124
  1.6 14.2 %collective-permute-start = (bf16[192,320]{0,1:T(8,128)(2,1)S(1)}, bf16[192,320]{0,1:T(8,128)(2,1)S(1)}, u32[]{:S(2)}, u32[]{:S(2)}) collective-permute-start(bf16[192,320]{0,1:T(8,128)(2,1)S(1)} %get-tuple-element.59), channel_id=1, source_target_pairs={{16,32},{48,64},{80,96},{112,128},{144,160},{176,192},{208,224},{2... | collective-permute-start | bytes 368648 | tf_op jit(solution)/shard_map/ppermute | solution.py:20
  6.5 9.3 %collective-permute-start.2 = (bf16[192,320]{0,1:T(8,128)(2,1)S(1)}, bf16[192,320]{0,1:T(8,128)(2,1)S(1)}, u32[]{:S(2)}, u32[]{:S(2)}) collective-permute-start(bf16[192,320]{0,1:T(8,128)(2,1)S(1)} %get-tuple-element.60), channel_id=1, source_target_pairs={{1,2},{3,4},{5,6},{7,8},{9,10},{11,12},{13,14},{2,1},{4,3},{6,5},{... | collective-permute-start | bytes 368648 | tf_op jit(solution)/shard_map/ppermute | solution.py:20
  7.2 9.8 %collective-permute-start.3 = (bf16[192,320]{0,1:T(8,128)(2,1)S(1)}, bf16[192,320]{0,1:T(8,128)(2,1)S(1)}, u32[]{:S(2)}, u32[]{:S(2)}) collective-permute-start(bf16[192,320]{0,1:T(8,128)(2,1)S(1)} %get-tuple-element.61), channel_id=1, source_target_pairs={{0,1},{2,3},{4,5},{6,7},{8,9},{10,11},{12,13},{14,15},{1,0},{3,2},... | collective-permute-start | bytes 368648 | tf_op jit(solution)/shard_map/ppermute | solution.py:20
  12.9 4.1 %collective-permute-start.1 = (bf16[192,320]{0,1:T(8,128)(2,1)S(1)}, bf16[192,320]{0,1:T(8,128)(2,1)S(1)}, u32[]{:S(2)}, u32[]{:S(2)}) collective-permute-start(bf16[192,320]{0,1:T(8,128)(2,1)S(1)} %get-tuple-element.62), channel_id=1, source_target_pairs={{0,16},{32,48},{64,80},{96,112},{128,144},{160,176},{192,208},{224... | collective-permute-start | bytes 368648 | tf_op jit(solution)/shard_map/ppermute | solution.py:20
  15.8 1.3 copy-start.24
  15.8 1.2 copy-start.25
  18.3 1.5 copy-start.30
  19.8 50.6 %copy-start.2 = (f32[192,320]{0,1:T(8,128)}, f32[192,320]{0,1:T(8,128)S(1)}, u32[]{:S(2)}) copy-start(f32[192,320]{0,1:T(8,128)S(1)} %get-tuple-element.34) | copy-start | bytes 737284
  19.8 50.6 %copy-start.5 = (f32[192,320]{0,1:T(8,128)}, f32[192,320]{0,1:T(8,128)S(1)}, u32[]{:S(2)}) copy-start(f32[192,320]{0,1:T(8,128)S(1)} %get-tuple-element.35) | copy-start | bytes 737284
  19.8 50.6 %copy-start.8 = (f32[192,320]{0,1:T(8,128)}, f32[192,320]{0,1:T(8,128)S(1)}, u32[]{:S(2)}) copy-start(f32[192,320]{0,1:T(8,128)S(1)} %get-tuple-element.45) | copy-start | bytes 737284
  19.8 50.6 %copy-start.11 = (f32[192,320]{0,1:T(8,128)}, f32[192,320]{0,1:T(8,128)S(1)}, u32[]{:S(2)}) copy-start(f32[192,320]{0,1:T(8,128)S(1)} %get-tuple-element.46) | copy-start | bytes 737284
  34.4 28.2 %all-to-all-start.1 = ((bf16[16,16,320]{2,1,0:T(8,128)(2,1)}), bf16[16,16,320]{2,1,0:T(8,128)(2,1)S(1)}, u32[]{:S(2)}, u32[]{:S(2)}) async-start(bf16[16,16,320]{2,1,0:T(8,128)(2,1)} %broadcast_in_dim.80), calls=%async_computation.1 | async-start | bytes 393216 | tf_op jit(solution)/shard_map/all_to_all | solution.py:25
  51.3 21.0 %copy-start.23 = (bf16[32,512]{0,1:T(8,128)(2,1)}, bf16[32,512]{0,1:T(8,128)(2,1)S(1)}, u32[]{:S(2)}) copy-start(bf16[32,512]{0,1:T(8,128)(2,1)S(1)} %copy.17) | copy-start | bytes 98308
  51.3 21.9 %copy-start.28 = (bf16[8,768]{1,0:T(8,128)(2,1)}, bf16[8,768]{1,0:T(8,128)(2,1)S(1)}, u32[]{:S(2)}) copy-start(bf16[8,768]{1,0:T(8,128)(2,1)S(1)} %get-tuple-element.64) | copy-start | bytes 36868
  62.9 9.4 %collective-permute-start.4 = (f32[16,320]{1,0:T(8,128)S(1)}, f32[16,320]{1,0:T(8,128)S(1)}, u32[]{:S(2)}, u32[]{:S(2)}) collective-permute-start(f32[16,320]{1,0:T(8,128)S(1)} %slice_select_fusion.1), channel_id=1, source_target_pairs={{0,16},{16,0},{1,17},{17,1},{2,18},{18,2},{3,19},{19,3},{4,20},{20... | collective-permute-start | bytes 61448 | tf_op jit(solution)/shard_map/ppermute | solution.py:124
  73.7 10.0 %collective-permute-start.5 = (bf16[192,320]{0,1:T(8,128)(2,1)S(1)}, bf16[192,320]{0,1:T(8,128)(2,1)S(1)}, u32[]{:S(2)}, u32[]{:S(2)}) collective-permute-start(bf16[192,320]{0,1:T(8,128)(2,1)S(1)} %get-tuple-element.55), channel_id=1, source_target_pairs={{16,32},{48,64},{80,96},{112,128},{144,160},{176,192},{208,224},{2... | collective-permute-start | bytes 368648 | tf_op jit(solution)/shard_map/ppermute | solution.py:20
  77.0 6.8 %collective-permute-start.7 = (bf16[192,320]{0,1:T(8,128)(2,1)S(1)}, bf16[192,320]{0,1:T(8,128)(2,1)S(1)}, u32[]{:S(2)}, u32[]{:S(2)}) collective-permute-start(bf16[192,320]{0,1:T(8,128)(2,1)S(1)} %get-tuple-element.56), channel_id=1, source_target_pairs={{1,2},{3,4},{5,6},{7,8},{9,10},{11,12},{13,14},{2,1},{4,3},{6,5},{... | collective-permute-start | bytes 368648 | tf_op jit(solution)/shard_map/ppermute | solution.py:20
  77.6 6.9 %collective-permute-start.8 = (bf16[192,320]{0,1:T(8,128)(2,1)S(1)}, bf16[192,320]{0,1:T(8,128)(2,1)S(1)}, u32[]{:S(2)}, u32[]{:S(2)}) collective-permute-start(bf16[192,320]{0,1:T(8,128)(2,1)S(1)} %get-tuple-element.57), channel_id=1, source_target_pairs={{0,1},{2,3},{4,5},{6,7},{8,9},{10,11},{12,13},{14,15},{1,0},{3,2},... | collective-permute-start | bytes 368648 | tf_op jit(solution)/shard_map/ppermute | solution.py:20
  81.8 3.3 %collective-permute-start.6 = (bf16[192,320]{0,1:T(8,128)(2,1)S(1)}, bf16[192,320]{0,1:T(8,128)(2,1)S(1)}, u32[]{:S(2)}, u32[]{:S(2)}) collective-permute-start(bf16[192,320]{0,1:T(8,128)(2,1)S(1)} %get-tuple-element.58), channel_id=1, source_target_pairs={{0,16},{32,48},{64,80},{96,112},{128,144},{160,176},{192,208},{224... | collective-permute-start | bytes 368648 | tf_op jit(solution)/shard_map/ppermute | solution.py:20
  85.1 1.0 copy-start.3
  85.1 1.1 copy-start.6
  85.1 1.2 copy-start.9
  85.1 1.3 copy-start.12
  87.4 11.7 %collective-permute-start.9 = (bf16[192,320]{0,1:T(8,128)(2,1)S(1)}, bf16[192,320]{0,1:T(8,128)(2,1)S(1)}, u32[]{:S(2)}, u32[]{:S(2)}) collective-permute-start(bf16[192,320]{0,1:T(8,128)(2,1)S(1)} %get-tuple-element.51), channel_id=1, source_target_pairs={{16,32},{48,64},{80,96},{112,128},{144,160},{176,192},{208,224},{2... | collective-permute-start | bytes 368648 | tf_op jit(solution)/shard_map/ppermute | solution.py:20
  91.2 7.9 %collective-permute-start.11 = (bf16[192,320]{0,1:T(8,128)(2,1)S(1)}, bf16[192,320]{0,1:T(8,128)(2,1)S(1)}, u32[]{:S(2)}, u32[]{:S(2)}) collective-permute-start(bf16[192,320]{0,1:T(8,128)(2,1)S(1)} %get-tuple-element.52), channel_id=1, source_target_pairs={{1,2},{3,4},{5,6},{7,8},{9,10},{11,12},{13,14},{2,1},{4,3},{6,5},{... | collective-permute-start | bytes 368648 | tf_op jit(solution)/shard_map/ppermute | solution.py:20
  91.9 8.0 %collective-permute-start.12 = (bf16[192,320]{0,1:T(8,128)(2,1)S(1)}, bf16[192,320]{0,1:T(8,128)(2,1)S(1)}, u32[]{:S(2)}, u32[]{:S(2)}) collective-permute-start(bf16[192,320]{0,1:T(8,128)(2,1)S(1)} %get-tuple-element.53), channel_id=1, source_target_pairs={{0,1},{2,3},{4,5},{6,7},{8,9},{10,11},{12,13},{14,15},{1,0},{3,2},... | collective-permute-start | bytes 368648 | tf_op jit(solution)/shard_map/ppermute | solution.py:20
  97.2 3.3 %collective-permute-start.10 = (bf16[192,320]{0,1:T(8,128)(2,1)S(1)}, bf16[192,320]{0,1:T(8,128)(2,1)S(1)}, u32[]{:S(2)}, u32[]{:S(2)}) collective-permute-start(bf16[192,320]{0,1:T(8,128)(2,1)S(1)} %get-tuple-element.54), channel_id=1, source_target_pairs={{0,16},{32,48},{64,80},{96,112},{128,144},{160,176},{192,208},{224... | collective-permute-start | bytes 368648 | tf_op jit(solution)/shard_map/ppermute | solution.py:20
  100.8 1.7 copy-start.19
  100.8 1.7 copy-start.21
  100.8 51.2 %copy-start.17 = (f32[192,320]{0,1:T(8,128)}, f32[192,320]{0,1:T(8,128)S(1)}, u32[]{:S(2)}) copy-start(f32[192,320]{0,1:T(8,128)S(1)} %get-tuple-element.27) | copy-start | bytes 737284
  103.3 15.2 %all-to-all-start.2 = ((f32[16,16,320]{2,1,0:T(8,128)}), f32[16,16,320]{2,1,0:T(8,128)S(1)}, u32[]{:S(2)}, u32[]{:S(2)}) async-start(f32[16,16,320]{2,1,0:T(8,128)} %broadcast_in_dim.82), calls=%async_computation.2 | async-start | bytes 786432 | tf_op jit(solution)/shard_map/all_to_all | solution.py:25
  109.2 42.8 %copy-start.15 = (f32[192,320]{0,1:T(8,128)S(1)}, f32[192,320]{0,1:T(8,128)}, u32[]{:S(2)}) copy-start(f32[192,320]{0,1:T(8,128)} %copy-done.14) | copy-start | bytes 737284
  120.7 19.6 %all-to-all-start.3 = ((bf16[16,24,320]{2,1,0:T(8,128)(2,1)}), bf16[16,24,320]{2,1,0:T(8,128)(2,1)}, u32[]{:S(2)}, u32[]{:S(2)}) async-start(bf16[16,24,320]{2,1,0:T(8,128)(2,1)} %broadcast_in_dim.84), calls=%async_computation.3 | async-start | bytes 589824 | tf_op jit(solution)/shard_map/all_to_all | solution.py:25
  142.3 12.7 %copy-start.29 = (bf16[8,768]{1,0:T(8,128)(2,1)S(1)}, bf16[8,768]{1,0:T(8,128)(2,1)}, u32[]{:S(2)}) copy-start(bf16[8,768]{1,0:T(8,128)(2,1)} %copy-done.28) | copy-start | bytes 36868
  142.4 11.8 %collective-permute-start.13 = (f32[24,320]{1,0:T(8,128)S(1)}, f32[24,320]{1,0:T(8,128)S(1)}, u32[]{:S(2)}, u32[]{:S(2)}) collective-permute-start(f32[24,320]{1,0:T(8,128)S(1)} %pad_maximum_fusion.2), channel_id=1, source_target_pairs={{0,16},{16,0},{1,17},{17,1},{2,18},{18,2},{3,19},{19,3},{4,20},{20... | collective-permute-start | bytes 92168 | tf_op jit(solution)/shard_map/ppermute | solution.py:124
  155.6 9.5 %collective-permute-start.14 = (bf16[192,320]{0,1:T(8,128)(2,1)S(1)}, bf16[192,320]{0,1:T(8,128)(2,1)S(1)}, u32[]{:S(2)}, u32[]{:S(2)}) collective-permute-start(bf16[192,320]{0,1:T(8,128)(2,1)S(1)} %get-tuple-element.47), channel_id=1, source_target_pairs={{16,32},{48,64},{80,96},{112,128},{144,160},{176,192},{208,224},{2... | collective-permute-start | bytes 368648 | tf_op jit(solution)/shard_map/ppermute | solution.py:20
  158.5 6.6 %collective-permute-start.16 = (bf16[192,320]{0,1:T(8,128)(2,1)S(1)}, bf16[192,320]{0,1:T(8,128)(2,1)S(1)}, u32[]{:S(2)}, u32[]{:S(2)}) collective-permute-start(bf16[192,320]{0,1:T(8,128)(2,1)S(1)} %get-tuple-element.48), channel_id=1, source_target_pairs={{1,2},{3,4},{5,6},{7,8},{9,10},{11,12},{13,14},{2,1},{4,3},{6,5},{... | collective-permute-start | bytes 368648 | tf_op jit(solution)/shard_map/ppermute | solution.py:20
  159.2 7.1 %collective-permute-start.17 = (bf16[192,320]{0,1:T(8,128)(2,1)S(1)}, bf16[192,320]{0,1:T(8,128)(2,1)S(1)}, u32[]{:S(2)}, u32[]{:S(2)}) collective-permute-start(bf16[192,320]{0,1:T(8,128)(2,1)S(1)} %get-tuple-element.49), channel_id=1, source_target_pairs={{0,1},{2,3},{4,5},{6,7},{8,9},{10,11},{12,13},{14,15},{1,0},{3,2},... | collective-permute-start | bytes 368648 | tf_op jit(solution)/shard_map/ppermute | solution.py:20
  163.1 3.3 %collective-permute-start.15 = (bf16[192,320]{0,1:T(8,128)(2,1)S(1)}, bf16[192,320]{0,1:T(8,128)(2,1)S(1)}, u32[]{:S(2)}, u32[]{:S(2)}) collective-permute-start(bf16[192,320]{0,1:T(8,128)(2,1)S(1)} %get-tuple-element.50), channel_id=1, source_target_pairs={{0,16},{32,48},{64,80},{96,112},{128,144},{160,176},{192,208},{224... | collective-permute-start | bytes 368648 | tf_op jit(solution)/shard_map/ppermute | solution.py:20
  166.4 1.1 copy-start.7
  166.4 1.2 copy-start.10
  166.4 1.3 copy-start.13
  166.4 1.4 copy-start.16
  166.4 1.4 copy-start.18
  166.4 1.5 copy-start.20
  166.4 1.6 copy-start.22
  (6 other events, 4.0 us)

commit v3 on v2

--- a/solution.py
+++ b/solution.py
@@ -30,27 +30,30 @@
     return [vec[k * width : (k + 1) * width] for k in range(4)]
 
 
-def neighbours(parts):
-    west, east, south, north = parts
+def beside_x(west, east):
     left = lax.axis_index(GX) % 2 == 0
+    far = traded(jnp.where(left, west, east), GX, 1)
+    near = traded(jnp.where(left, east, west), GX, 0)
+    return (jnp.where(left, far, near), jnp.where(left, near, far))
+
+
+def beside_y(south, north):
     lower = lax.axis_index(GY) % 2 == 0
-    far_y = traded(jnp.where(lower, south, north), GY, 1)
-    near_y = traded(jnp.where(lower, north, south), GY, 0)
-    far_x = traded(jnp.where(left, west, east), GX, 1)
-    near_x = traded(jnp.where(left, east, west), GX, 0)
-    return (
-        jnp.where(left, far_x, near_x),
-        jnp.where(left, near_x, far_x),
-        jnp.where(lower, far_y, near_y),
-        jnp.where(lower, near_y, far_y),
-    )
-
-
-def assemble(vec):
-    others = neighbours(edges_of(vec.astype(jnp.bfloat16)))
+    far = traded(jnp.where(lower, south, north), GY, 1)
+    near = traded(jnp.where(lower, north, south), GY, 0)
+    return (jnp.where(lower, far, near), jnp.where(lower, near, far))
+
+
+def joined(vec, others):
     return jnp.concatenate(
         [mine + other.astype(vec.dtype) for mine, other in zip(edges_of(vec), others)], axis=0
     )
+
+
+def assemble(vec):
+    west, east, south, north = edges_of(vec.astype(jnp.bfloat16))
+    y = beside_y(south, north)
+    return joined(vec, (*beside_x(west, east), *y))
 
 
 def halves(value):
@@ -99,14 +102,29 @@
     ).astype(jnp.float32)
     weights = jnp.repeat(edge_w, width)[:, None]
     own = aggregate[0, 0]
-    second_inv = lax.dynamic_slice_in_dim(level2_inverse[0], row * count, count, 0)
-    third_inv = lax.dynamic_slice_in_dim(
-        level3_inverse, (col - core) * block, cores * block, 0
-    )
-    third_inv = third_inv.reshape(cores * block, cols_total // cores, cores, block)
-    third_inv = lax.dynamic_index_in_dim(third_inv, core, 2, keepdims=False)
+    before, after = (jnp.maximum(row - 1, 0), jnp.minimum(row + 1, rows_total - 1))
+    second_inv = jnp.concatenate(
+        [
+            lax.dynamic_slice_in_dim(level2_inverse[0], k * count, count, 0)
+            for k in (row, before, after)
+        ],
+        axis=0,
+    )
     planes = cols_total // cores
-    third_first = third_inv.reshape(cores * block, planes * block)
+    columns = level3_inverse.reshape(cols_total * block, planes, cores, block)
+    columns = lax.dynamic_index_in_dim(columns, core, 2, keepdims=False)
+    left = jnp.maximum(col - core - 1, 0)
+    right = jnp.minimum(col - core + cores, cols_total - 1)
+    third_inv = jnp.concatenate(
+        [
+            lax.dynamic_slice_in_dim(columns, left * block, block, 0),
+            lax.dynamic_slice_in_dim(columns, (col - core) * block, cores * block, 0),
+            lax.dynamic_slice_in_dim(columns, right * block, block, 0),
+        ],
+        axis=0,
+    )
+    near = (cores + 1) * block
+    third_first = third_inv.reshape(-1, planes * block)
     adders = jnp.array([[1, 0, 1, 0, 0, 0, 0, 0], [0, 1, 0, 1, 0, 0, 0, 0]], jnp.bfloat16)
     adders = jnp.pad(adders, ((0, 6), (block, 0)))
     third_dots = jnp.concatenate(
@@ -119,6 +137,26 @@
     basis_hi, basis_lo = halves(basis)
     spread = jnp.concatenate([basis_hi, basis_lo, basis_hi], axis=0).T
     tags = jnp.broadcast_to(own.astype(jnp.float32), (count, 128 - rows % 128))
+    label = jnp.broadcast_to(own.astype(jnp.bfloat16), (total, 8))
+    depth = spread.shape[1]
+    first = jnp.concatenate([load_here.astype(jnp.bfloat16), spread, label], axis=1)
+    west, east, south, north = edges_of(first)
+    others_y = beside_y(south, north)
+    others = (*beside_x(west, east), *others_y)
+    rhs = weights * joined(load_here, [other[:, :rows] for other in others])
+    west_own, east_own = (other[0, rows + depth].astype(jnp.int32) for other in others[:2])
+    across = jnp.concatenate([other[:, rows : rows + depth] for other in others], axis=0)
+    edge_at = lax.broadcasted_iota(jnp.int32, (total, depth), 0) // width
+    lift = jnp.concatenate(
+        [spread, *(jnp.where(edge_at == k, across, jnp.zeros_like(across)) for k in range(4))],
+        axis=1,
+    )
+
+    def chosen(third, at, agg):
+        value = third[at : at + count]
+        for k in range(1, NAGG):
+            value = jnp.where(agg == k, third[at + k * count : at + (k + 1) * count], value)
+        return value
 
     def swapped(value):
         return lax.ppermute(value, CORE, [(0, 1), (1, 0)])
@@ -132,6 +170,8 @@
             group = group[:, :, :rows]
         else:
             group = copies(jnp.concatenate([primal, extra], axis=0), GY)
+        west, east, south, north = edges_of(local.astype(jnp.bfloat16))
+        others_y = beside_y(south, north)
         group, found = (group[:, :count], group[:, count:])
         summed = [
             jnp.sum(jnp.where(members == label, group, 0.0), axis=0) for label in range(NAGG)
@@ -146,19 +186,33 @@
         everyone = copies(jnp.concatenate(summed, axis=0).astype(jnp.bfloat16), DEPTH)
         second = times_high(second_inv, group.reshape(rows_total * count, rows))
         parts = times(third_inv, everyone.reshape(-1, rows))
-        here, there = (parts[:block], parts[block : 2 * block])
-        kept = jnp.where(core == 0, here, there)
-        sent = jnp.where(core == 0, there, here)
-        dots = parts[2 * block :]
+        second_hi, second_lo = halves(second[:count])
+        others_x = beside_x(
+            jnp.concatenate([west, second_hi, second_lo], axis=0),
+            jnp.concatenate([east, second_hi, second_lo], axis=0),
+        )
+        second_west, second_east = (
+            (other[width : width + count].astype(jnp.float32) + other[width + count :].astype(jnp.float32))
+            for other in others_x
+        )
+        local = joined(local, (*(other[:width] for other in others_x), *others_y))
+        dots = parts[near + block :]
+        kept = jnp.where(core == 0, parts[:near], parts[block : near + block])
+        sent = jnp.where(core == 0, parts[block : near + block], parts[:near])
         got = swapped(jnp.concatenate([sent, dots], axis=0))
-        third = kept + got[:block]
-        third_own = third[:count]
-        for label in range(1, NAGG):
-            third_own = jnp.where(own == label, third[label * count : (label + 1) * count], third_own)
-        coarse_hi, coarse_lo = halves(second + third_own)
-        stacked = jnp.concatenate([coarse_hi, coarse_hi, coarse_lo], axis=0)
-        full = local + times(spread, stacked)
-        return (assemble(weights * full), members, dots + got[block:])
+        third = kept + got[:near]
+        aggs = members[:, 0, 0]
+        coarse = [
+            second[:count] + chosen(third, block, own),
+            second_west + chosen(third, 0, west_own),
+            second_east + chosen(third, 2 * block, east_own),
+            second[count : 2 * count] + chosen(third, block, aggs[before]),
+            second[2 * count :] + chosen(third, block, aggs[after]),
+        ]
+        coarse_hi, coarse_lo = halves(jnp.stack(coarse))
+        stacked = jnp.concatenate([coarse_hi, coarse_hi, coarse_lo], axis=1)
+        full = local + times(lift, stacked.reshape(5 * depth, rows))
+        return (weights * full, members, dots + got[near:])
 
     def apply(vec):
         return times(stiff, vec.astype(jnp.bfloat16))
@@ -166,7 +220,6 @@
     def inner(left, right):
         return jnp.sum(left * right, axis=0)
 
-    rhs = weights * assemble(load_here)
     zero, members, _ = precondition(rhs, None, None)
     image = apply(zero)
     dots = jnp.stack([inner(rhs, zero), inner(zero, image)])

time: 207 us -> 187 us (0.903)
  waiting for transfers between devices: 36.9 us -> 13.2 us
  blocking collectives: 45.2 us -> 28.9 us
  starting transfers between devices: 89.6 us -> 96 us
  other arithmetic: 10.8 us -> 15.6 us
  local copies, waits for them, and re-layouts: 10.5 us -> 13.6 us
  between operations: 1.49 us -> 4.5 us
  matrix products: 11.4 us -> 14 us
    all_to_all x3 -> x4, waiting for transfers between devices: 31.7 us -> 6.5 us  [copies(): return lax.all_to_all(parts, axis, split_axis=0, concat_axis=0, tiled=True)]
    all_to_all x3 -> x2, blocking collectives: 45.2 us -> 28.9 us  [copies(): return lax.all_to_all(parts, axis, split_axis=0, concat_axis=0, tiled=True)]
    select_n x6 -> x13, other arithmetic: 0.66 us -> 8.16 us  [the longest x3 2.08 us: beside_x(): return (jnp.where(left, far, near), jnp.where(left, near, far))]
    ppermute x16, starting transfers between devices: 44.2 us -> 50.4 us  [traded(): return lax.ppermute(value, axis, pairs + [(b, a) for a, b in pairs])]
    all_to_all x3 -> x4, starting transfers between devices: 28.3 us -> 33.9 us  [copies(): return lax.all_to_all(parts, axis, split_axis=0, concat_axis=0, tiled=True)]
    ppermute x2, starting transfers between devices: 17.1 us -> 11.7 us  [swapped(): return lax.ppermute(value, CORE, [(0, 1), (1, 0)])]
    dot_general x8, matrix products: 7.7 us -> 10.6 us  [times(): lax.dot_general(left, right, (((1,), (0,)), ((), ())), preferred_element_...]
    unnamed x67 -> x68, local copies, waits for them, and re-layouts: 5.01 us -> 5.13 us
  transfers between devices with their start and end apart: 21 -> 22, of which waited for: 10 -> 5; matrix products, arithmetic and copies ran while one was open for 4% -> 11% of each run, Pallas kernels for 0% -> 0%
where the time goes in v3:
time: 187 us; the launch traced here: 186 us
  starting transfers between devices  96 us (51%)
  blocking collectives  28.9 us (15%)
  other arithmetic  15.6 us (8%)
  matrix products  14 us (7%)
  local copies, waits for them, and re-layouts  13.6 us (7%)
  waiting for transfers between devices  13.2 us (7%)
  between operations  4.5 us (2%)
    ppermute x16, starting transfers between devices, traded(): return lax.ppermute(value, axis, pairs + [(b, a) for a, b in pairs])  50.4 us
    all_to_all x4, starting transfers between devices, copies(): return lax.all_to_all(parts, axis, split_axis=0, concat_axis=0, tiled=True)  33.9 us
    all_to_all x2, blocking collectives, copies(): return lax.all_to_all(parts, axis, split_axis=0, concat_axis=0, tiled=True)  28.9 us
    ppermute x2, starting transfers between devices, swapped(): return lax.ppermute(value, CORE, [(0, 1), (1, 0)])  11.7 us
    dot_general x8, matrix products, times(): lax.dot_general(left, right, (((1,), (0,)), ((), ())), preferred_element_...  10.6 us
    ppermute x16, waiting for transfers between devices, traded(): return lax.ppermute(value, axis, pairs + [(b, a) for a, b in pairs])  6.65 us
    all_to_all x4, waiting for transfers between devices, copies(): return lax.all_to_all(parts, axis, split_axis=0, concat_axis=0, tiled=True)  6.5 us
    unnamed x68, local copies, waits for them, and re-layouts  5.13 us
  transfers between devices with their start and end apart: 22, of which 5 were waited for; matrix products, arithmetic and copies ran while one was open for 11% of the time, Pallas kernels for 0%

profile of v3, /device:TPU:1, one launch (start us, length us, event | category | flops | bytes accessed | tf_op | source)
XLA Modules:
  0.0 185.7 jit_solution(14015282959301736513)
XLA Ops:
  1.7 1.6 copy.170
  3.6 0.8 broadcast_select_fusion.23
  4.4 4.9 %collective-permute-start = (bf16[192,352]{1,0:T(8,128)(2,1)}, bf16[192,352]{1,0:T(8,128)(2,1)}, u32[]{:S(2)}, u32[]{:S(2)}) collective-permute-start(bf16[192,352]{1,0:T(8,128)(2,1)} %get-tuple-element.53), channel_id=1, source_target_pairs={{16,32},{48,64},{80,96},{112,128},{144,160},{176,192},{208,224},{2... | collective-permute-start | bytes 405512 | tf_op jit(solution)/shard_map/ppermute | solution.py:20
  9.3 1.3 collective-permute-start.2
  10.7 5.1 %collective-permute-start.3 = (bf16[192,352]{1,0:T(8,128)(2,1)S(1)}, bf16[192,352]{1,0:T(8,128)(2,1)}, u32[]{:S(2)}, u32[]{:S(2)}) collective-permute-start(bf16[192,352]{1,0:T(8,128)(2,1)S(1)} %get-tuple-element.55), channel_id=1, source_target_pairs={{0,1},{2,3},{4,5},{6,7},{8,9},{10,11},{12,13},{14,15},{1,0},{3,2},... | collective-permute-start | bytes 405512 | tf_op jit(solution)/shard_map/ppermute | solution.py:20
  15.8 2.0 %collective-permute-start.1 = (bf16[192,352]{1,0:T(8,128)(2,1)}, bf16[192,352]{1,0:T(8,128)(2,1)}, u32[]{:S(2)}, u32[]{:S(2)}) collective-permute-start(bf16[192,352]{1,0:T(8,128)(2,1)} %get-tuple-element.56), channel_id=1, source_target_pairs={{0,16},{32,48},{64,80},{96,112},{128,144},{160,176},{192,208},{224... | collective-permute-start | bytes 405512 | tf_op jit(solution)/shard_map/ppermute | solution.py:20
  17.8 1.3 copy.169
  19.3 0.8 dynamic-slice_bitcast_fusion.5
  20.5 1.0 broadcast_select_fusion.21
  22.9 1.0 broadcast_select_fusion.17
  25.4 0.9 slice_add_fusion.15
  26.3 2.1 %convolution_bitcast_fusion.7 = f32[8,320]{1,0:T(8,128)S(1)} fusion(f32[1,1,8,768]{3,2,1,0:T(8,128)S(1)} %copy-done.21, f32[192,320]{1,0:T(8,128)} %get-tuple-element.40, f32[192,320]{1,0:T(8,128)S(1)} %get-tuple-element.38, f32[192,320]{1,0:T(8,128)} %get-tuple-element.39, f32[192,320]{1,0:T(8,128)S(1)} %get-tuple-element.37, f32[768]{0:T(1024)S(1)} %mul.122), kind=kOutput, calls=%fused_computation.25 | convolution fusion | flops 24576000 | bytes 1020928 | tf_op jit(solution)/shard_map/dot_general | solution.py:71
  29.1 5.7 %all-to-all-start = ((f32[16,8,384]{2,1,0:T(8,128)}), f32[16,8,384]{2,1,0:T(8,128)S(1)}, u32[]{:S(2)}, u32[]{:S(2)}) async-start(f32[16,8,384]{2,1,0:T(8,128)} %broadcast_in_dim.78), calls=%async_computation | async-start | bytes 393216 | tf_op jit(solution)/shard_map/all_to_all | solution.py:25
  34.8 2.9 %fusion.63 = (bf16[768,320]{1,0:T(8,128)(2,1)S(1)}, f32[768,320]{1,0:T(8,128)}) fusion(f32[192,320]{1,0:T(8,128)} %get-tuple-element.40, f32[192,320]{1,0:T(8,128)S(1)} %get-tuple-element.38, f32[192,320]{1,0:T(8,128)} %get-tuple-element.39, f32[192,320]{1,0:T(8,128)S(1)} %get-tuple-element.37, f32[768]{0:T(1024)S(1)} %mul.122, ...), kind=kOutput, calls=%fused_computation.203 | convolution fusion | flops 378961920 | bytes 3640320 | tf_op jit(solution)/shard_map/dot_general | solution.py:65
  38.5 1.3 collective-permute-start.6
  39.8 5.0 %collective-permute-start.7 = (bf16[192,320]{1,0:T(8,128)(2,1)}, bf16[192,320]{1,0:T(8,128)(2,1)}, u32[]{:S(2)}, u32[]{:S(2)}) collective-permute-start(bf16[192,320]{1,0:T(8,128)(2,1)} %get-tuple-element.52), channel_id=1, source_target_pairs={{0,1},{2,3},{4,5},{6,7},{8,9},{10,11},{12,13},{14,15},{1,0},{3,2},... | collective-permute-start | bytes 368648 | tf_op jit(solution)/shard_map/ppermute | solution.py:20
  46.5 14.0 %all-to-all-start.1 = ((bf16[16,16,320]{2,1,0:T(8,128)(2,1)}), bf16[16,16,320]{2,1,0:T(8,128)(2,1)S(1)}, u32[]{:S(2)}, u32[]{:S(2)}) async-start(bf16[16,16,320]{2,1,0:T(8,128)(2,1)} %broadcast_in_dim.84), calls=%async_computation.1 | async-start | bytes 393216 | tf_op jit(solution)/shard_map/all_to_all | solution.py:25
  60.8 0.8 broadcast_select_fusion.6
  61.6 3.8 %collective-permute-start.5 = (bf16[208,320]{1,0:T(8,128)(2,1)}, bf16[208,320]{1,0:T(8,128)(2,1)}, u32[]{:S(2)}, u32[]{:S(2)}) collective-permute-start(bf16[208,320]{1,0:T(8,128)(2,1)} %get-tuple-element.65), channel_id=1, source_target_pairs={{0,16},{32,48},{64,80},{96,112},{128,144},{160,176},{192,208},{224... | collective-permute-start | bytes 399368 | tf_op jit(solution)/shard_map/ppermute | solution.py:20
  65.4 3.4 %collective-permute-start.4 = (bf16[208,320]{1,0:T(8,128)(2,1)}, bf16[208,320]{1,0:T(8,128)(2,1)}, u32[]{:S(2)}, u32[]{:S(2)}) collective-permute-start(bf16[208,320]{1,0:T(8,128)(2,1)} %get-tuple-element.66), channel_id=1, source_target_pairs={{16,32},{48,64},{80,96},{112,128},{144,160},{176,192},{208,224},{2... | collective-permute-start | bytes 399368 | tf_op jit(solution)/shard_map/ppermute | solution.py:20
  68.8 1.8 fusion.17
  73.1 0.8 collective-permute-done.4
  73.9 1.0 broadcast_select_fusion.4
  75.2 5.0 %collective-permute-start.8 = (f32[48,320]{1,0:T(8,128)S(1)}, f32[48,320]{1,0:T(8,128)S(1)}, u32[]{:S(2)}, u32[]{:S(2)}) collective-permute-start(f32[48,320]{1,0:T(8,128)S(1)} %slice_select_fusion.1), channel_id=1, source_target_pairs={{0,16},{16,0},{1,17},{17,1},{2,18},{18,2},{3,19},{19,3},{4,20},{20... | collective-permute-start | bytes 184328 | tf_op jit(solution)/shard_map/ppermute | solution.py:162
  80.3 1.1 slice_add_fusion.9
  82.9 2.3 %multiply_reduce_fusion.1 = (f32[320]{0:T(512)S(1)}, f32[320]{0:T(512)S(1)}, bf16[768,320]{1,0:T(8,128)(2,1)S(1)}, f32[768,320]{1,0:T(8,128)S(1)}) fusion(f32[768,320]{1,0:T(8,128)S(1)} %fusion.2, f32[192,320]{1,0:T(8,128)} %get-tuple-element.40, f32[192,320]{1,0:T(8,128)S(1)} %copy-done.9, f32[192,320]{1,0:T(8,128)} %get-tuple-element.39, ...), kind=kOutput, calls=%fused_computation.20 | convolution fusion | flops 379944320 | bytes 4625920 | tf_op jit(solution)/shard_map/dot_general | solution.py:65
  85.4 3.5 %collective-permute-start.9 = (bf16[192,320]{1,0:T(8,128)(2,1)S(1)}, bf16[192,320]{1,0:T(8,128)(2,1)S(1)}, u32[]{:S(2)}, u32[]{:S(2)}) collective-permute-start(bf16[192,320]{1,0:T(8,128)(2,1)S(1)} %get-tuple-element.45), channel_id=1, source_target_pairs={{16,32},{48,64},{80,96},{112,128},{144,160},{176,192},{208,224},{2... | collective-permute-start | bytes 368648 | tf_op jit(solution)/shard_map/ppermute | solution.py:20
  89.5 5.2 %collective-permute-start.12 = (bf16[192,320]{1,0:T(8,128)(2,1)S(1)}, bf16[192,320]{1,0:T(8,128)(2,1)S(1)}, u32[]{:S(2)}, u32[]{:S(2)}) collective-permute-start(bf16[192,320]{1,0:T(8,128)(2,1)S(1)} %get-tuple-element.47), channel_id=1, source_target_pairs={{0,1},{2,3},{4,5},{6,7},{8,9},{10,11},{12,13},{14,15},{1,0},{3,2},... | collective-permute-start | bytes 368648 | tf_op jit(solution)/shard_map/ppermute | solution.py:20
  94.8 1.9 %collective-permute-start.10 = (bf16[192,320]{1,0:T(8,128)(2,1)S(1)}, bf16[192,320]{1,0:T(8,128)(2,1)S(1)}, u32[]{:S(2)}, u32[]{:S(2)}) collective-permute-start(bf16[192,320]{1,0:T(8,128)(2,1)S(1)} %get-tuple-element.48), channel_id=1, source_target_pairs={{0,16},{32,48},{64,80},{96,112},{128,144},{160,176},{192,208},{224... | collective-permute-start | bytes 368648 | tf_op jit(solution)/shard_map/ppermute | solution.py:20
  98.8 0.8 convolution_bitcast_fusion.6
  100.4 6.6 %all-to-all-start.2 = ((f32[16,16,320]{2,1,0:T(8,128)}), f32[16,16,320]{2,1,0:T(8,128)S(1)}, u32[]{:S(2)}, u32[]{:S(2)}) async-start(f32[16,16,320]{2,1,0:T(8,128)} %broadcast_in_dim.86), calls=%async_computation.2 | async-start | bytes 786432 | tf_op jit(solution)/shard_map/all_to_all | solution.py:25
  107.1 1.9 %fusion.64 = (bf16[768,320]{1,0:T(8,128)(2,1)S(1)}, f32[768,320]{1,0:T(8,128)S(1)}) fusion(f32[192,320]{1,0:T(8,128)} %copy-done.15, f32[192,320]{1,0:T(8,128)} %copy-done.17, f32[192,320]{1,0:T(8,128)S(1)} %get-tuple-element.25, f32[192,320]{1,0:T(8,128)S(1)} %get-tuple-element.24, f32[768]{0:T(1024)S(1)} %copy-done.30, ...), kind=kOutput, calls=%fused_computation.204 | convolution fusion | flops 378961920 | bytes 3640320 | tf_op jit(solution)/shard_map/dot_general | solution.py:65
  109.0 0.8 broadcast_select_fusion.11
  109.8 6.5 %all-to-all-done.2 = f32[16,16,320]{2,1,0:T(8,128)S(1)} async-done(((f32[16,16,320]{2,1,0:T(8,128)}), f32[16,16,320]{2,1,0:T(8,128)S(1)}, u32[]{:S(2)}, u32[]{:S(2)}) %all-to-all-start.2) | async-done | bytes 327712 | tf_op jit(solution)/shard_map/all_to_all | solution.py:25
  117.3 7.6 %all-to-all-start.3 = ((bf16[16,24,320]{2,1,0:T(8,128)(2,1)}), bf16[16,24,320]{2,1,0:T(8,128)(2,1)S(1)}, u32[]{:S(2)}, u32[]{:S(2)}) async-start(bf16[16,24,320]{2,1,0:T(8,128)(2,1)} %broadcast_in_dim.88), calls=%async_computation.3 | async-start | bytes 589824 | tf_op jit(solution)/shard_map/all_to_all | solution.py:25
  125.2 4.1 %collective-permute-start.15 = (bf16[208,320]{1,0:T(8,128)(2,1)S(1)}, bf16[208,320]{1,0:T(8,128)(2,1)S(1)}, u32[]{:S(2)}, u32[]{:S(2)}) collective-permute-start(bf16[208,320]{1,0:T(8,128)(2,1)S(1)} %get-tuple-element.63), channel_id=1, source_target_pairs={{0,16},{32,48},{64,80},{96,112},{128,144},{160,176},{192,208},{224... | collective-permute-start | bytes 399368 | tf_op jit(solution)/shard_map/ppermute | solution.py:20
  129.3 3.4 %collective-permute-start.14 = (bf16[208,320]{1,0:T(8,128)(2,1)S(1)}, bf16[208,320]{1,0:T(8,128)(2,1)S(1)}, u32[]{:S(2)}, u32[]{:S(2)}) collective-permute-start(bf16[208,320]{1,0:T(8,128)(2,1)S(1)} %get-tuple-element.64), channel_id=1, source_target_pairs={{16,32},{48,64},{80,96},{112,128},{144,160},{176,192},{208,224},{2... | collective-permute-start | bytes 399368 | tf_op jit(solution)/shard_map/ppermute | solution.py:20
  132.7 1.3 collective-permute-start.16
  134.0 3.4 %collective-permute-start.17 = (bf16[192,320]{1,0:T(8,128)(2,1)}, bf16[192,320]{1,0:T(8,128)(2,1)}, u32[]{:S(2)}, u32[]{:S(2)}) collective-permute-start(bf16[192,320]{1,0:T(8,128)(2,1)} %get-tuple-element.44), channel_id=1, source_target_pairs={{0,1},{2,3},{4,5},{6,7},{8,9},{10,11},{12,13},{14,15},{1,0},{3,2},... | collective-permute-start | bytes 368648 | tf_op jit(solution)/shard_map/ppermute | solution.py:20
  137.4 4.5 %collective-permute-done.14 = bf16[208,320]{1,0:T(8,128)(2,1)S(1)} collective-permute-done((bf16[208,320]{1,0:T(8,128)(2,1)S(1)}, bf16[208,320]{1,0:T(8,128)(2,1)S(1)}, u32[]{:S(2)}, u32[]{:S(2)}) %collective-permute-start.14) | collective-permute-done | bytes 133152 | tf_op jit(solution)/shard_map/ppermute | solution.py:20
  142.4 6.6 %collective-permute-start.13 = (f32[56,320]{1,0:T(8,128)S(1)}, f32[56,320]{1,0:T(8,128)S(1)}, u32[]{:S(2)}, u32[]{:S(2)}) collective-permute-start(f32[56,320]{1,0:T(8,128)S(1)} %pad_maximum_fusion.11), channel_id=1, source_target_pairs={{0,16},{16,0},{1,17},{17,1},{2,18},{18,2},{3,19},{19,3},{4,20},{20... | collective-permute-start | bytes 215048 | tf_op jit(solution)/shard_map/ppermute | solution.py:162
  149.1 1.2 slice_add_fusion.1
  151.0 1.8 multiply_reduce_fusion
  152.9 0.8 fusion.1
  153.9 11.0 %all_to_all.30 = f32[32,2,320]{2,1,0:T(2,128)S(1)} all-to-all(f32[32,2,320]{2,1,0:T(2,128)S(1)} %broadcast_in_dim.89), channel_id=1, replica_groups=mesh['gx_0'=16,'gx_1'=2,'gy_0'=4,'gy_1'=4] {'gx_1','gy_0','gy_1'}, dimensions={0} | all-to-all | bytes 163840 | tf_op jit(solution)/shard_map/all_to_all | solution.py:25
  165.0 17.9 %all_to_all.31 = f32[16,2,320]{2,1,0:T(2,128)S(1)} all-to-all(f32[16,2,320]{2,1,0:T(2,128)S(1)} %broadcast_in_dim.90), channel_id=1, replica_groups=mesh['gx_0'=16,'gx_1'=2,'gy_0'=4,'gy_1'=4] {'gx_0'}, dimensions={0} | all-to-all | bytes 81920 | tf_op jit(solution)/shard_map/all_to_all | solution.py:25
  183.0 1.4 add_bitcast_fusion
  184.4 1.3 copy.180
  (170 shorter events, 15.6 us)
Async XLA Ops:
  0.0 34.8 %copy-start = (bf16[1,1,768,768]{3,2,1,0:T(8,128)(2,1)S(1)}, bf16[1,1,768,768]{3,2,1,0:T(8,128)(2,1)}, u32[]{:S(2)}) copy-start(bf16[1,1,768,768]{3,2,1,0:T(8,128)(2,1)} %param.10) | copy-start | bytes 3538948
  4.4 16.1 %collective-permute-start = (bf16[192,352]{1,0:T(8,128)(2,1)}, bf16[192,352]{1,0:T(8,128)(2,1)}, u32[]{:S(2)}, u32[]{:S(2)}) collective-permute-start(bf16[192,352]{1,0:T(8,128)(2,1)} %get-tuple-element.53), channel_id=1, source_target_pairs={{16,32},{48,64},{80,96},{112,128},{144,160},{176,192},{208,224},{2... | collective-permute-start | bytes 405512 | tf_op jit(solution)/shard_map/ppermute | solution.py:20
  9.3 13.5 %collective-permute-start.2 = (bf16[192,352]{1,0:T(8,128)(2,1)}, bf16[192,352]{1,0:T(8,128)(2,1)}, u32[]{:S(2)}, u32[]{:S(2)}) collective-permute-start(bf16[192,352]{1,0:T(8,128)(2,1)} %get-tuple-element.54), channel_id=1, source_target_pairs={{1,2},{3,4},{5,6},{7,8},{9,10},{11,12},{13,14},{2,1},{4,3},{6,5},{... | collective-permute-start | bytes 405512 | tf_op jit(solution)/shard_map/ppermute | solution.py:20
  10.7 12.2 %collective-permute-start.3 = (bf16[192,352]{1,0:T(8,128)(2,1)S(1)}, bf16[192,352]{1,0:T(8,128)(2,1)}, u32[]{:S(2)}, u32[]{:S(2)}) collective-permute-start(bf16[192,352]{1,0:T(8,128)(2,1)S(1)} %get-tuple-element.55), channel_id=1, source_target_pairs={{0,1},{2,3},{4,5},{6,7},{8,9},{10,11},{12,13},{14,15},{1,0},{3,2},... | collective-permute-start | bytes 405512 | tf_op jit(solution)/shard_map/ppermute | solution.py:20
  15.8 4.7 %collective-permute-start.1 = (bf16[192,352]{1,0:T(8,128)(2,1)}, bf16[192,352]{1,0:T(8,128)(2,1)}, u32[]{:S(2)}, u32[]{:S(2)}) collective-permute-start(bf16[192,352]{1,0:T(8,128)(2,1)} %get-tuple-element.56), channel_id=1, source_target_pairs={{0,16},{32,48},{64,80},{96,112},{128,144},{160,176},{192,208},{224... | collective-permute-start | bytes 405512 | tf_op jit(solution)/shard_map/ppermute | solution.py:20
  20.4 14.4 %copy-start.28 = (f32[768]{0:T(1024)}, f32[768]{0:T(1024)S(1)}, u32[]{:S(2)}) copy-start(f32[768]{0:T(1024)S(1)} %mul.122) | copy-start | bytes 9220
  26.3 8.5 %copy-start.8 = (f32[192,320]{1,0:T(8,128)}, f32[192,320]{1,0:T(8,128)S(1)}, u32[]{:S(2)}) copy-start(f32[192,320]{1,0:T(8,128)S(1)} %get-tuple-element.38) | copy-start | bytes 737284
  26.3 55.6 %copy-start.6 = (f32[192,320]{1,0:T(8,128)}, f32[192,320]{1,0:T(8,128)S(1)}, u32[]{:S(2)}) copy-start(f32[192,320]{1,0:T(8,128)S(1)} %get-tuple-element.37) | copy-start | bytes 737284
  29.1 15.8 %all-to-all-start = ((f32[16,8,384]{2,1,0:T(8,128)}), f32[16,8,384]{2,1,0:T(8,128)S(1)}, u32[]{:S(2)}, u32[]{:S(2)}) async-start(f32[16,8,384]{2,1,0:T(8,128)} %broadcast_in_dim.78), calls=%async_computation | async-start | bytes 393216 | tf_op jit(solution)/shard_map/all_to_all | solution.py:25
  38.5 41.7 %collective-permute-start.6 = (bf16[192,320]{1,0:T(8,128)(2,1)}, bf16[192,320]{1,0:T(8,128)(2,1)}, u32[]{:S(2)}, u32[]{:S(2)}) collective-permute-start(bf16[192,320]{1,0:T(8,128)(2,1)} %get-tuple-element.49), channel_id=1, source_target_pairs={{1,2},{3,4},{5,6},{7,8},{9,10},{11,12},{13,14},{2,1},{4,3},{6,5},{... | collective-permute-start | bytes 368648 | tf_op jit(solution)/shard_map/ppermute | solution.py:20
  39.8 40.4 %collective-permute-start.7 = (bf16[192,320]{1,0:T(8,128)(2,1)}, bf16[192,320]{1,0:T(8,128)(2,1)}, u32[]{:S(2)}, u32[]{:S(2)}) collective-permute-start(bf16[192,320]{1,0:T(8,128)(2,1)} %get-tuple-element.52), channel_id=1, source_target_pairs={{0,1},{2,3},{4,5},{6,7},{8,9},{10,11},{12,13},{14,15},{1,0},{3,2},... | collective-permute-start | bytes 368648 | tf_op jit(solution)/shard_map/ppermute | solution.py:20
  45.6 14.9 %copy-start.24 = (pred[16]{0:T(512)(128)(4,1)}, pred[16]{0:T(512)(128)(4,1)S(1)}, u32[]{:S(2)}) copy-start(pred[16]{0:T(512)(128)(4,1)S(1)} %get-tuple-element.12) | copy-start | bytes 52
  45.6 14.9 %copy-start.26 = (pred[16]{0:T(512)(128)(4,1)}, pred[16]{0:T(512)(128)(4,1)S(1)}, u32[]{:S(2)}) copy-start(pred[16]{0:T(512)(128)(4,1)S(1)} %get-tuple-element.13) | copy-start | bytes 52
  46.5 28.5 %all-to-all-start.1 = ((bf16[16,16,320]{2,1,0:T(8,128)(2,1)}), bf16[16,16,320]{2,1,0:T(8,128)(2,1)S(1)}, u32[]{:S(2)}, u32[]{:S(2)}) async-start(bf16[16,16,320]{2,1,0:T(8,128)(2,1)} %broadcast_in_dim.84), calls=%async_computation.1 | async-start | bytes 393216 | tf_op jit(solution)/shard_map/all_to_all | solution.py:25
  61.6 11.5 %collective-permute-start.5 = (bf16[208,320]{1,0:T(8,128)(2,1)}, bf16[208,320]{1,0:T(8,128)(2,1)}, u32[]{:S(2)}, u32[]{:S(2)}) collective-permute-start(bf16[208,320]{1,0:T(8,128)(2,1)} %get-tuple-element.65), channel_id=1, source_target_pairs={{0,16},{32,48},{64,80},{96,112},{128,144},{160,176},{192,208},{224... | collective-permute-start | bytes 399368 | tf_op jit(solution)/shard_map/ppermute | solution.py:20
  65.4 8.6 %collective-permute-start.4 = (bf16[208,320]{1,0:T(8,128)(2,1)}, bf16[208,320]{1,0:T(8,128)(2,1)}, u32[]{:S(2)}, u32[]{:S(2)}) collective-permute-start(bf16[208,320]{1,0:T(8,128)(2,1)} %get-tuple-element.66), channel_id=1, source_target_pairs={{16,32},{48,64},{80,96},{112,128},{144,160},{176,192},{208,224},{2... | collective-permute-start | bytes 399368 | tf_op jit(solution)/shard_map/ppermute | solution.py:20
  71.1 10.4 %copy-start.19 = (bf16[768,120]{1,0:T(8,128)(2,1)}, bf16[768,120]{1,0:T(8,128)(2,1)S(1)}, u32[]{:S(2)}) copy-start(bf16[768,120]{1,0:T(8,128)(2,1)S(1)} %concatenate.80) | copy-start | bytes 552964
  71.2 9.1 %copy-start.1 = (f32[768,320]{1,0:T(8,128)S(1)}, f32[768,320]{1,0:T(8,128)}, u32[]{:S(2)}) copy-start(f32[768,320]{1,0:T(8,128)} %get-tuple-element.91) | copy-start | bytes 2949124
  75.2 6.2 %collective-permute-start.8 = (f32[48,320]{1,0:T(8,128)S(1)}, f32[48,320]{1,0:T(8,128)S(1)}, u32[]{:S(2)}, u32[]{:S(2)}) collective-permute-start(f32[48,320]{1,0:T(8,128)S(1)} %slice_select_fusion.1), channel_id=1, source_target_pairs={{0,16},{16,0},{1,17},{17,1},{2,18},{18,2},{3,19},{19,3},{4,20},{20... | collective-permute-start | bytes 184328 | tf_op jit(solution)/shard_map/ppermute | solution.py:162
  82.9 2.4 %copy-start.2 = (f32[768,320]{1,0:T(8,128)}, f32[768,320]{1,0:T(8,128)S(1)}, u32[]{:S(2)}) copy-start(f32[768,320]{1,0:T(8,128)S(1)} %fusion.2) | copy-start | bytes 2949124
  85.4 11.4 %collective-permute-start.9 = (bf16[192,320]{1,0:T(8,128)(2,1)S(1)}, bf16[192,320]{1,0:T(8,128)(2,1)S(1)}, u32[]{:S(2)}, u32[]{:S(2)}) collective-permute-start(bf16[192,320]{1,0:T(8,128)(2,1)S(1)} %get-tuple-element.45), channel_id=1, source_target_pairs={{16,32},{48,64},{80,96},{112,128},{144,160},{176,192},{208,224},{2... | collective-permute-start | bytes 368648 | tf_op jit(solution)/shard_map/ppermute | solution.py:20
  88.9 7.9 %collective-permute-start.11 = (bf16[192,320]{1,0:T(8,128)(2,1)S(1)}, bf16[192,320]{1,0:T(8,128)(2,1)S(1)}, u32[]{:S(2)}, u32[]{:S(2)}) collective-permute-start(bf16[192,320]{1,0:T(8,128)(2,1)S(1)} %get-tuple-element.46), channel_id=1, source_target_pairs={{1,2},{3,4},{5,6},{7,8},{9,10},{11,12},{13,14},{2,1},{4,3},{6,5},{... | collective-permute-start | bytes 368648 | tf_op jit(solution)/shard_map/ppermute | solution.py:20
  89.5 7.7 %collective-permute-start.12 = (bf16[192,320]{1,0:T(8,128)(2,1)S(1)}, bf16[192,320]{1,0:T(8,128)(2,1)S(1)}, u32[]{:S(2)}, u32[]{:S(2)}) collective-permute-start(bf16[192,320]{1,0:T(8,128)(2,1)S(1)} %get-tuple-element.47), channel_id=1, source_target_pairs={{0,1},{2,3},{4,5},{6,7},{8,9},{10,11},{12,13},{14,15},{1,0},{3,2},... | collective-permute-start | bytes 368648 | tf_op jit(solution)/shard_map/ppermute | solution.py:20
  94.8 3.3 %collective-permute-start.10 = (bf16[192,320]{1,0:T(8,128)(2,1)S(1)}, bf16[192,320]{1,0:T(8,128)(2,1)S(1)}, u32[]{:S(2)}, u32[]{:S(2)}) collective-permute-start(bf16[192,320]{1,0:T(8,128)(2,1)S(1)} %get-tuple-element.48), channel_id=1, source_target_pairs={{0,16},{32,48},{64,80},{96,112},{128,144},{160,176},{192,208},{224... | collective-permute-start | bytes 368648 | tf_op jit(solution)/shard_map/ppermute | solution.py:20
  98.2 2.2 %copy-start.15 = (f32[192,320]{1,0:T(8,128)}, f32[192,320]{1,0:T(8,128)S(1)}, u32[]{:S(2)}) copy-start(f32[192,320]{1,0:T(8,128)S(1)} %get-tuple-element.33) | copy-start | bytes 737284
  98.2 2.2 %copy-start.17 = (f32[192,320]{1,0:T(8,128)}, f32[192,320]{1,0:T(8,128)S(1)}, u32[]{:S(2)}) copy-start(f32[192,320]{1,0:T(8,128)S(1)} %get-tuple-element.34) | copy-start | bytes 737284
  98.2 8.9 %copy-start.11 = (f32[192,320]{1,0:T(8,128)}, f32[192,320]{1,0:T(8,128)S(1)}, u32[]{:S(2)}) copy-start(f32[192,320]{1,0:T(8,128)S(1)} %get-tuple-element.24) | copy-start | bytes 737284
  98.2 8.9 %copy-start.13 = (f32[192,320]{1,0:T(8,128)}, f32[192,320]{1,0:T(8,128)S(1)}, u32[]{:S(2)}) copy-start(f32[192,320]{1,0:T(8,128)S(1)} %get-tuple-element.25) | copy-start | bytes 737284
  99.6 7.5 %copy-start.30 = (f32[768]{0:T(1024)S(1)}, f32[768]{0:T(1024)}, u32[]{:S(2)}) copy-start(f32[768]{0:T(1024)} %copy-done.28) | copy-start | bytes 9220
  100.4 15.9 %all-to-all-start.2 = ((f32[16,16,320]{2,1,0:T(8,128)}), f32[16,16,320]{2,1,0:T(8,128)S(1)}, u32[]{:S(2)}, u32[]{:S(2)}) async-start(f32[16,16,320]{2,1,0:T(8,128)} %broadcast_in_dim.86), calls=%async_computation.2 | async-start | bytes 786432 | tf_op jit(solution)/shard_map/all_to_all | solution.py:25
  109.0 7.3 %copy-start.25 = (pred[16]{0:T(512)(128)(4,1)S(1)}, pred[16]{0:T(512)(128)(4,1)}, u32[]{:S(2)}) copy-start(pred[16]{0:T(512)(128)(4,1)} %copy-done.24) | copy-start | bytes 52
  109.0 7.3 %copy-start.27 = (pred[16]{0:T(512)(128)(4,1)S(1)}, pred[16]{0:T(512)(128)(4,1)}, u32[]{:S(2)}) copy-start(pred[16]{0:T(512)(128)(4,1)} %copy-done.26) | copy-start | bytes 52
  116.5 25.5 %copy-start.23 = (bf16[8,24]{0,1:T(8,128)(2,1)S(1)}, bf16[8,24]{0,1:T(8,128)(2,1)}, u32[]{:S(2)}) copy-start(bf16[8,24]{0,1:T(8,128)(2,1)} %constant.189) | copy-start | bytes 1156
  117.3 24.7 %all-to-all-start.3 = ((bf16[16,24,320]{2,1,0:T(8,128)(2,1)}), bf16[16,24,320]{2,1,0:T(8,128)(2,1)S(1)}, u32[]{:S(2)}, u32[]{:S(2)}) async-start(bf16[16,24,320]{2,1,0:T(8,128)(2,1)} %broadcast_in_dim.88), calls=%async_computation.3 | async-start | bytes 589824 | tf_op jit(solution)/shard_map/all_to_all | solution.py:25
  125.2 12.2 %collective-permute-start.15 = (bf16[208,320]{1,0:T(8,128)(2,1)S(1)}, bf16[208,320]{1,0:T(8,128)(2,1)S(1)}, u32[]{:S(2)}, u32[]{:S(2)}) collective-permute-start(bf16[208,320]{1,0:T(8,128)(2,1)S(1)} %get-tuple-element.63), channel_id=1, source_target_pairs={{0,16},{32,48},{64,80},{96,112},{128,144},{160,176},{192,208},{224... | collective-permute-start | bytes 399368 | tf_op jit(solution)/shard_map/ppermute | solution.py:20
  129.3 12.7 %collective-permute-start.14 = (bf16[208,320]{1,0:T(8,128)(2,1)S(1)}, bf16[208,320]{1,0:T(8,128)(2,1)S(1)}, u32[]{:S(2)}, u32[]{:S(2)}) collective-permute-start(bf16[208,320]{1,0:T(8,128)(2,1)S(1)} %get-tuple-element.64), channel_id=1, source_target_pairs={{16,32},{48,64},{80,96},{112,128},{144,160},{176,192},{208,224},{2... | collective-permute-start | bytes 399368 | tf_op jit(solution)/shard_map/ppermute | solution.py:20
  132.7 16.3 %collective-permute-start.16 = (bf16[192,320]{1,0:T(8,128)(2,1)}, bf16[192,320]{1,0:T(8,128)(2,1)}, u32[]{:S(2)}, u32[]{:S(2)}) collective-permute-start(bf16[192,320]{1,0:T(8,128)(2,1)} %get-tuple-element.41), channel_id=1, source_target_pairs={{1,2},{3,4},{5,6},{7,8},{9,10},{11,12},{13,14},{2,1},{4,3},{6,5},{... | collective-permute-start | bytes 368648 | tf_op jit(solution)/shard_map/ppermute | solution.py:20
  134.0 15.0 %collective-permute-start.17 = (bf16[192,320]{1,0:T(8,128)(2,1)}, bf16[192,320]{1,0:T(8,128)(2,1)}, u32[]{:S(2)}, u32[]{:S(2)}) collective-permute-start(bf16[192,320]{1,0:T(8,128)(2,1)} %get-tuple-element.44), channel_id=1, source_target_pairs={{0,1},{2,3},{4,5},{6,7},{8,9},{10,11},{12,13},{14,15},{1,0},{3,2},... | collective-permute-start | bytes 368648 | tf_op jit(solution)/shard_map/ppermute | solution.py:20
  142.4 8.0 %collective-permute-start.13 = (f32[56,320]{1,0:T(8,128)S(1)}, f32[56,320]{1,0:T(8,128)S(1)}, u32[]{:S(2)}, u32[]{:S(2)}) collective-permute-start(f32[56,320]{1,0:T(8,128)S(1)} %pad_maximum_fusion.11), channel_id=1, source_target_pairs={{0,16},{16,0},{1,17},{17,1},{2,18},{18,2},{3,19},{19,3},{4,20},{20... | collective-permute-start | bytes 215048 | tf_op jit(solution)/shard_map/ppermute | solution.py:162
  149.0 1.5 copy-start.3
  149.1 1.5 copy-start.10
  149.1 1.6 copy-start.12
  149.1 1.7 copy-start.14
  149.1 1.8 copy-start.16
  149.1 1.8 copy-start.18
  149.1 1.9 %copy-start.20 = (bf16[768,120]{1,0:T(8,128)(2,1)S(1)}, bf16[768,120]{1,0:T(8,128)(2,1)}, u32[]{:S(2)}) copy-start(bf16[768,120]{1,0:T(8,128)(2,1)} %copy-done.19) | copy-start | bytes 552964
  151.0 1.9 %copy-start.32 = (bf16[1,1,768,768]{3,2,1,0:T(8,128)(2,1)S(1)}, bf16[1,1,768,768]{3,2,1,0:T(8,128)(2,1)}, u32[]{:S(2)}) copy-start(bf16[1,1,768,768]{3,2,1,0:T(8,128)(2,1)} %param.9) | copy-start | bytes 3538948
  152.9 30.1 %copy-start.4 = (f32[768,320]{1,0:T(8,128)S(1)}, f32[768,320]{1,0:T(8,128)}, u32[]{:S(2)}) copy-start(f32[768,320]{1,0:T(8,128)} %copy-done.2) | copy-start | bytes 2949124
  (7 other events, 7.8 us)
